TPU v7x, 32 devices: a whole 2x2x4 slice. The times are simulated.
32 devices in a mesh: outer: 4 (over y, x), inner: 8 (over z, core).
Axes of the slice: x: 2, y: 2, z: 4, core: 2. Of those that a mesh axis runs over, the one named last changes fastest.
Arguments:
- queries: bfloat16 [2048, 1024], P(('outer', 'inner')), may hold values from -8 to 8
- key_rows: bfloat16 [2048, 1024], P(('outer', 'inner')), may hold values from -8 to 8
- value_rows: bfloat16 [2048, 1024], P(('outer', 'inner')), may hold values from -6 to 6
Outputs:
- attended: float32 [2048, 1024], P(('outer', 'inner'))
All inputs are finite; a program needn't handle non-finite values.
Results may differ from a plain program's by a relative error of at most 0.0021.
Values may be sent and summed in bfloat16 or wider, within the bound.
A program may use at most 64 MiB of HBM per device.

v0:
```python
import math
from functools import partial, reduce

import jax
import jax.numpy as jnp
import numpy as np
from jax import lax
from jax.experimental import pallas as pl
from jax.experimental.pallas import tpu as pltpu
from jax.sharding import PartitionSpec as P

HEADS = 16


FLOOR_SCORE = -1e30


def divisor_block(length, limit):
    extent = min(length, limit)
    while length % extent:
        extent -= 1
    return extent


def fresh_state(count, rows, width):
    return (
        jnp.full((count, rows), FLOOR_SCORE, jnp.float32),
        jnp.zeros((count, rows), jnp.float32),
        jnp.zeros((count, rows, width), jnp.float32),
    )


def finish_state(state):
    row_max, denominator, summed = state
    return (summed / denominator[..., None], row_max + jnp.log(denominator))


def online_step(state, query_rows, query_rank, key_rows, value_rows, key_rank):
    row_max, denominator, summed = state
    scale = query_rows.shape[-1] ** (-0.5)
    scores = (
        jnp.einsum("inh,ibh->inb", query_rows, key_rows, preferred_element_type=jnp.float32) * scale
    )
    scores = jnp.where(key_rank[None, None, :] <= query_rank[None, :, None], scores, FLOOR_SCORE)
    new_max = jnp.maximum(row_max, jnp.max(scores, axis=2))
    weights = jnp.exp(scores - new_max[..., None])
    rescale = jnp.exp(row_max - new_max)
    denominator = denominator * rescale + jnp.sum(weights, axis=2)
    summed = summed * rescale[..., None] + jnp.einsum(
        "inb,ibh->inh", weights.astype(jnp.bfloat16), value_rows, preferred_element_type=jnp.float32
    )
    return (new_max, denominator, summed)


def attend_keys(state, query_rows, query_rank, key_rows, value_rows, key_rank, stop=None):
    length = key_rows.shape[1]
    block = divisor_block(length, 512)

    def advance(index, carry):
        start = index * block
        piece_keys = lax.dynamic_slice_in_dim(key_rows, start, block, 1)
        piece_values = lax.dynamic_slice_in_dim(value_rows, start, block, 1)
        piece_rank = lax.dynamic_slice_in_dim(key_rank, start, block, 0)
        return online_step(carry, query_rows, query_rank, piece_keys, piece_values, piece_rank)

    upper = length // block if stop is None else stop
    return lax.fori_loop(0, upper, advance, state)


def attend(query_rows, query_rank, key_rows, value_rows, key_rank):
    count, length, width = query_rows.shape
    block = divisor_block(length, 512)
    steps = length // block
    query_split = query_rows.reshape(count, steps, block, width).swapaxes(0, 1)
    rank_split = query_rank.reshape(steps, block)

    def one_block(pieces):
        state = attend_keys(
            fresh_state(count, block, width),
            pieces[0],
            pieces[1],
            key_rows,
            value_rows,
            key_rank,
            pieces[2] + 1,
        )
        return finish_state(state)

    outputs, lses = lax.map(
        one_block, (query_split, rank_split, jnp.arange(steps, dtype=jnp.int32))
    )
    return (
        outputs.swapaxes(0, 1).reshape(count, length, width),
        lses.swapaxes(0, 1).reshape(count, length),
    )


def merge_levels(parts):
    row_max = reduce(jnp.maximum, [lse for _, lse in parts])
    weights = [jnp.exp(lse - row_max) for _, lse in parts]
    denominator = reduce(jnp.add, weights)
    summed = reduce(
        jnp.add, [weight[..., None] * output for weight, (output, _) in zip(weights, parts)]
    )
    return (summed / denominator[..., None], row_max + jnp.log(denominator))


def on_device(queries, key_rows, value_rows):
    tokens, features = queries.shape
    heads = HEADS
    width = features // heads
    outer_count = lax.axis_size("outer")
    inner_count = lax.axis_size("inner")
    outer_index = lax.axis_index("outer")
    inner_index = lax.axis_index("inner")
    per_device = 4 * heads // inner_count
    quarter = tokens // 4
    sixteenth = tokens // 16
    class_len = quarter * inner_count
    far_len = sixteenth * inner_count

    def to_items(array):
        return (
            array.reshape(quarter, 4, heads, width)
            .transpose(2, 1, 0, 3)
            .reshape(4 * heads, quarter, width)
        )

    local_ranks = jnp.arange(tokens, dtype=jnp.int32)
    head_major = [
        a.reshape(tokens, heads, width).transpose(1, 0, 2) for a in (queries, key_rows, value_rows)
    ]
    near_out, near_lse = attend(
        head_major[0], local_ranks, head_major[1], head_major[2], local_ranks
    )
    near_out = near_out.transpose(1, 0, 2)
    near_lse = near_lse.T
    item_index = inner_index * per_device + jnp.arange(per_device, dtype=jnp.int32)
    band = item_index // 16
    far_query_rank = outer_index * far_len + jnp.arange(far_len, dtype=jnp.int32)
    pick = np.array(
        [head * 16 + head // 4 * 4 + residue for head in range(heads) for residue in range(4)],
        np.int32,
    )

    def to_sixteen(array):
        spread = (
            array.reshape(sixteenth, 16, heads, width)
            .transpose(2, 1, 0, 3)
            .reshape(16 * heads, sixteenth, width)
        )
        return jnp.take(spread, pick, axis=0)

    gathered_k, gathered_v = (
        lax.all_gather(to_sixteen(key_rows), "outer", axis=1, tiled=True),
        lax.all_gather(to_sixteen(value_rows), "outer", axis=1, tiled=True),
    )
    mid_q, mid_k, mid_v, far_k, far_v = (
        lax.all_to_all(to_items(queries), "inner", split_axis=0, concat_axis=1, tiled=True),
        lax.all_to_all(to_items(key_rows), "inner", split_axis=0, concat_axis=1, tiled=True),
        lax.all_to_all(to_items(value_rows), "inner", split_axis=0, concat_axis=1, tiled=True),
        lax.all_to_all(gathered_k, "inner", split_axis=0, concat_axis=1, tiled=True),
        lax.all_to_all(gathered_v, "inner", split_axis=0, concat_axis=1, tiled=True),
    )
    split = mid_q.reshape(per_device, far_len, 4, width)
    picker = jnp.broadcast_to(band[:, None, None, None], (per_device, far_len, 1, width))
    far_q = jnp.take_along_axis(split, picker, axis=2)[:, :, 0, :]
    position = jnp.arange(far_k.shape[1], dtype=jnp.int32)
    far_key_rank = (
        position // sixteenth % outer_count * far_len
        + position // (outer_count * sixteenth) * sixteenth
        + position % sixteenth
    )
    far_state = attend_keys(
        fresh_state(per_device, far_len, width), far_q, far_query_rank, far_k, far_v, far_key_rank
    )
    far_out, far_lse = finish_state(far_state)
    class_ranks = jnp.arange(class_len, dtype=jnp.int32)
    mid_out, mid_lse = attend(mid_q, class_ranks, mid_k, mid_v, class_ranks)
    back_mid, back_mid_lse, back_far, back_far_lse = (
        lax.all_to_all(mid_out, "inner", split_axis=1, concat_axis=0, tiled=True),
        lax.all_to_all(mid_lse, "inner", split_axis=1, concat_axis=0, tiled=True),
        lax.all_to_all(far_out, "inner", split_axis=1, concat_axis=0, tiled=True),
        lax.all_to_all(far_lse, "inner", split_axis=1, concat_axis=0, tiled=True),
    )
    selector = np.array(
        [[band_index == head // 4 for band_index in range(4)] for head in range(heads)]
    )
    spread_out = jnp.where(
        selector[:, :, None, None, None], back_far.reshape(heads, 1, 4, sixteenth, width), 0.0
    )
    spread_lse = jnp.where(
        selector[:, :, None, None], back_far_lse.reshape(heads, 1, 4, sixteenth), FLOOR_SCORE
    )
    far_placed = (
        spread_out.reshape(heads, 16, sixteenth, width)
        .transpose(2, 1, 0, 3)
        .reshape(tokens, heads, width)
    )
    far_placed_lse = (
        spread_lse.reshape(heads, 16, sixteenth).transpose(2, 1, 0).reshape(tokens, heads)
    )
    placed = (
        back_mid.reshape(heads, 4, quarter, width)
        .transpose(2, 1, 0, 3)
        .reshape(tokens, heads, width)
    )
    placed_lse = back_mid_lse.reshape(heads, 4, quarter).transpose(2, 1, 0).reshape(tokens, heads)
    combined, _ = merge_levels(
        [(near_out, near_lse), (placed, placed_lse), (far_placed, far_placed_lse)]
    )
    return combined.reshape(tokens, features)


def fused_kernel(
    dims, q_ref, k_ref, v_ref, out_ref, q_held, k_held, v_held, q_buf, k_buf, v_buf, far_k, far_v, pick_k, pick_v, ready, ready_half, landed,
    in_send, in_recv, far_send, far_recv, back_send, back_recv, cross_send, cross_recv, own_sem, own_back, held_sem,
):
    inner, outer, tokens, slab, width, block = dims
    group = tokens * inner
    far_len = group // 4
    per_slab = slab // width
    me = lax.axis_index("inner")
    mine = lax.axis_index("outer")
    band = me * per_slab // 4
    sources = (k_ref, v_ref, q_ref)
    held = (k_held, v_held, q_held)
    half = inner // 2
    order = range(group // block)
    buffers = (k_buf, v_buf, q_buf)

    def columns(index):
        return pl.ds(pl.multiple_of(index * slab, slab), slab)

    def rows(index):
        return pl.ds(pl.multiple_of(index * tokens, tokens), tokens)

    def inbound(which, peer, owner):
        return pltpu.make_async_remote_copy(
            src_ref=held[which].at[:, columns(peer)],
            dst_ref=buffers[which].at[rows(owner), :],
            send_sem=in_send.at[which, peer],
            recv_sem=in_recv.at[which, owner],
            device_id={"inner": peer},
            device_id_type=pl.DeviceIdType.MESH,
        )

    def farbound(which, peer, owner):
        return pltpu.make_async_remote_copy(
            src_ref=(pick_k, pick_v)[which],
            dst_ref=(far_k, far_v)[which].at[owner],
            send_sem=far_send.at[which, peer],
            recv_sem=far_recv.at[which, owner],
            device_id={"outer": peer},
            device_id_type=pl.DeviceIdType.MESH,
        )

    def backbound(peer, owner):
        return pltpu.make_async_remote_copy(
            src_ref=ready.at[rows(peer), :],
            dst_ref=out_ref.at[:, columns(owner)],
            send_sem=back_send.at[peer],
            recv_sem=back_recv.at[owner],
            device_id={"inner": peer},
            device_id_type=pl.DeviceIdType.MESH,
        )

    def crossbound(peer, owner):
        return pltpu.make_async_remote_copy(
            src_ref=ready_half.at[rows(peer), :],
            dst_ref=landed.at[:, columns(owner)],
            send_sem=cross_send.at[peer],
            recv_sem=cross_recv.at[owner],
            device_id={"inner": peer},
            device_id_type=pl.DeviceIdType.MESH,
        )

    def near(peer):
        return (me // half == peer // half) & (me != peer)

    own_in = [
        pltpu.make_async_copy(
            sources[which].at[:, columns(me)], buffers[which].at[rows(me), :], own_sem.at[which]
        )
        for which in range(3)
    ]
    own_held = [
        pltpu.make_async_copy(sources[which], held[which], held_sem.at[which]) for which in range(3)
    ]
    for copy in own_held + own_in:
        copy.start()
    barrier = pltpu.get_barrier_semaphore()
    for step in range(1, inner):
        pl.semaphore_signal(
            barrier, inc=1, device_id={"inner": lax.rem(me + step, inner)},
            device_id_type=pl.DeviceIdType.MESH,
        )
    for step in range(1, outer):
        pl.semaphore_signal(
            barrier, inc=1, device_id={"outer": lax.rem(mine + step, outer)},
            device_id_type=pl.DeviceIdType.MESH,
        )
    pl.semaphore_wait(barrier, inner + outer - 2)

    for which in range(3):
        own_held[which].wait()
        for step in range(1, inner):
            inbound(which, lax.rem(me + step, inner), me).start()

    for other in range(outer - 1):

        @pl.when(mine <= other)
        def _():
            far_k[other] = jnp.zeros((far_len, slab), jnp.bfloat16)
            far_v[other] = jnp.zeros((far_len, slab), jnp.bfloat16)

    query_at = lax.broadcasted_iota(jnp.int32, (block, block), 0)
    key_at = lax.broadcasted_iota(jnp.int32, (block, block), 1)
    levels = (query_at % 4 == key_at % 4).astype(jnp.int32) + (
        (query_at % 16 == key_at % 16) & (query_at % 16 // 4 == band)
    ).astype(jnp.int32)

    def log_count(count):
        return jnp.where(
            count == 0,
            FLOOR_SCORE,
            jnp.where(count == 1, 0.0, jnp.where(count == 2, 1.0, math.log2(3.0))),
        )

    below = log_count(levels)
    diagonal = log_count(
        jnp.where(
            key_at <= query_at, levels + (query_at // tokens == key_at // tokens).astype(jnp.int32), 0
        )
    )
    far_query = lax.broadcasted_iota(jnp.int32, (block, far_len), 0)
    far_key = lax.broadcasted_iota(jnp.int32, (block, far_len), 1)
    far_one = jnp.where(far_query % 16 == 4 * band + far_key % 4, 0.0, FLOOR_SCORE)
    far_table = jnp.concatenate(
        [jnp.where(other < mine, far_one, FLOOR_SCORE) for other in range(outer - 1)], axis=1
    )
    picked = lax.broadcasted_iota(jnp.int32, (far_len, group), 0)
    picker = jnp.where(
        lax.broadcasted_iota(jnp.int32, (far_len, group), 1)
        == picked // 4 * 16 + 4 * band + picked % 4,
        1.0,
        0.0,
    ).astype(jnp.bfloat16)

    def arrive(which):
        own_in[which].wait()
        for step in range(1, inner):
            inbound(which, me, lax.rem(me + step, inner)).wait_recv()

    for which in range(2):
        arrive(which)
        (pick_k, pick_v)[which][...] = jnp.dot(
            picker, buffers[which][...], preferred_element_type=jnp.float32
        ).astype(jnp.bfloat16)
        for other in range(1, outer):

            @pl.when(mine < other)
            def _():
                farbound(which, other, mine).start()

    factor = width ** (-0.5) * math.log2(math.e)
    lane_head = lax.broadcasted_iota(jnp.int32, (block, slab), 1) // width
    contract = (((1,), (1,)), ((), ()))

    def query_of(index, head):
        piece = q_buf[index * block : (index + 1) * block, :]
        return jnp.where(lane_head == head, piece, jnp.zeros_like(piece))

    own_in[2].wait()
    states = {}
    for index in order:
        for peer in range(index * block // tokens, (index + 1) * block // tokens):

            @pl.when(me != peer)
            def _():
                inbound(2, me, peer).wait_recv()

        reach = (index + 1) * block
        table = jnp.concatenate([below] * index + [diagonal], axis=1)
        for head in range(per_slab):
            scores = lax.dot_general(
                query_of(index, head), k_buf[:reach, :], contract,
                preferred_element_type=jnp.float32,
            )
            scores = scores * factor + table
            top = jnp.max(scores, axis=1, keepdims=True)
            weights = jnp.exp2(scores - top)
            total = jnp.sum(weights, axis=1, keepdims=True)
            summed = jnp.dot(
                weights.astype(jnp.bfloat16), v_buf[:reach, :], preferred_element_type=jnp.float32
            )
            states[index, head] = (top, total, summed)

    for other in range(outer - 1):

        @pl.when(mine > other)
        def _():
            farbound(0, mine, other).wait_recv()
            farbound(1, mine, other).wait_recv()

    far_keys = far_k[...].reshape((outer - 1) * far_len, slab)
    far_values = far_v[...].reshape((outer - 1) * far_len, slab)
    for index in order:
        result = None
        for head in range(per_slab):
            top, total, summed = states[index, head]
            scores = lax.dot_general(
                query_of(index, head), far_keys, contract, preferred_element_type=jnp.float32
            )
            scores = scores * factor + far_table
            new_top = jnp.maximum(top, jnp.max(scores, axis=1, keepdims=True))
            rescale = jnp.exp2(top - new_top)
            weights = jnp.exp2(scores - new_top)
            total = total * rescale + jnp.sum(weights, axis=1, keepdims=True)
            summed = summed * rescale + jnp.dot(
                weights.astype(jnp.bfloat16), far_values, preferred_element_type=jnp.float32
            )
            finished = summed / total
            result = finished if result is None else jnp.where(lane_head == head, finished, result)
        ready[index * block : (index + 1) * block, :] = result
        ready_half[index * block : (index + 1) * block, :] = result.astype(jnp.bfloat16)
        for peer in range(index * block // tokens, (index + 1) * block // tokens):

            @pl.when(me // half != peer // half)
            def _():
                crossbound(peer, me).start()

            @pl.when(near(peer))
            def _():
                backbound(peer, me).start()

            @pl.when(me == peer)
            def _():
                pltpu.make_async_copy(
                    ready.at[rows(peer), :], out_ref.at[:, columns(peer)], own_back
                ).start()

    for owner in range(inner):

        @pl.when(me // half != owner // half)
        def _():
            crossbound(me, owner).wait_recv()
            place = slice(owner * slab, (owner + 1) * slab)
            out_ref[:, place] = landed[:, place].astype(jnp.float32)

    for owner in range(inner):

        @pl.when(near(owner))
        def _():
            backbound(me, owner).wait_recv()

    pltpu.make_async_copy(ready.at[rows(me), :], out_ref.at[:, columns(me)], own_back).wait()
    for step in range(1, inner):
        peer = lax.rem(me + step, inner)
        for which in range(3):
            inbound(which, peer, me).wait_send()

        @pl.when(me // half != peer // half)
        def _():
            crossbound(peer, me).wait_send()

        @pl.when(near(peer))
        def _():
            backbound(peer, me).wait_send()

    for other in range(1, outer):

        @pl.when(mine < other)
        def _():
            farbound(0, other, mine).wait_send()
            farbound(1, other, mine).wait_send()


def fused(queries, key_rows, value_rows, block):
    tokens, features = queries.shape
    inner = lax.axis_size("inner")
    outer = lax.axis_size("outer")
    slab = features // inner
    group = tokens * inner
    far_len = group // 4
    any_space = pl.BlockSpec(memory_space=pl.ANY)
    dims = (inner, outer, tokens, slab, features // HEADS, block)
    return pl.pallas_call(
        partial(fused_kernel, dims),
        out_shape=pltpu.VMEM((tokens, features), jnp.float32),
        in_specs=[any_space] * 3,
        out_specs=pl.BlockSpec(memory_space=pltpu.VMEM),
        scratch_shapes=[
            pltpu.VMEM((tokens, features), jnp.bfloat16),
            pltpu.VMEM((tokens, features), jnp.bfloat16),
            pltpu.VMEM((tokens, features), jnp.bfloat16),
            pltpu.VMEM((group, slab), jnp.bfloat16),
            pltpu.VMEM((group, slab), jnp.bfloat16),
            pltpu.VMEM((group, slab), jnp.bfloat16),
            pltpu.VMEM((outer - 1, far_len, slab), jnp.bfloat16),
            pltpu.VMEM((outer - 1, far_len, slab), jnp.bfloat16),
            pltpu.VMEM((far_len, slab), jnp.bfloat16),
            pltpu.VMEM((far_len, slab), jnp.bfloat16),
            pltpu.VMEM((group, slab), jnp.float32),
            pltpu.VMEM((group, slab), jnp.bfloat16),
            pltpu.VMEM((tokens, features), jnp.bfloat16),
            pltpu.SemaphoreType.DMA((3, inner)),
            pltpu.SemaphoreType.DMA((3, inner)),
            pltpu.SemaphoreType.DMA((2, outer)),
            pltpu.SemaphoreType.DMA((2, outer)),
            pltpu.SemaphoreType.DMA((inner,)),
            pltpu.SemaphoreType.DMA((inner,)),
            pltpu.SemaphoreType.DMA((inner,)),
            pltpu.SemaphoreType.DMA((inner,)),
            pltpu.SemaphoreType.DMA((3,)),
            pltpu.SemaphoreType.DMA,
            pltpu.SemaphoreType.DMA((3,)),
        ],
        compiler_params=pltpu.CompilerParams(collective_id=0, has_side_effects=True),
    )(queries, key_rows, value_rows)


def device_program(queries, key_rows, value_rows):
    tokens, features = queries.shape
    inner = lax.axis_size("inner")
    outer = lax.axis_size("outer")
    group = tokens * inner
    block = 2 * tokens
    slab = features // inner
    per_slab = HEADS // inner
    fits = (
        HEADS % inner == 0
        and outer > 1
        and inner % 2 == 0
        and per_slab > 0
        and 4 % max(per_slab, 1) == 0
        and slab % 128 == 0
        and tokens % 16 == 0
        and group % block == 0
        and group <= 1024
        and (outer - 1) * group // 4 <= 1024
    )
    if fits:
        return fused(queries, key_rows, value_rows, block)
    return on_device(queries, key_rows, value_rows)


def solution(mesh):
    placed = (P(("outer", "inner"), None), P(("outer", "inner"), None), P(("outer", "inner"), None))
    return jax.shard_map(
        device_program,
        mesh=mesh,
        in_specs=placed,
        out_specs=P(("outer", "inner"), None),
        check_vma=False,
    )
```

profile of v0, /device:TPU:0, one launch (start us, length us, event | category | flops | bytes accessed | tf_op | source)
XLA Modules:
  0.0 23.4 jit_solution(1402807498613888160)
XLA Ops:
  0.0 22.7 %shard_map.37 = f32[64,1024]{1,0:T(8,128)S(1)} custom-call(bf16[64,1024]{1,0:T(8,128)(2,1)} %q_ref.1, bf16[64,1024]{1,0:T(8,128)(2,1)} %k_ref.1, bf16[64,1024]{1,0:T(8,128)(2,1)} %v_ref.1), custom_call_target="tpu_custom_call" | custom-call | tf_op jit(solution)/shard_map/pallas_call | solution.py:488
  22.7 0.7 %copy.5 = f32[64,1024]{1,0:T(8,128)} copy(f32[64,1024]{1,0:T(8,128)S(1)} %shard_map.37) | data formatting | bytes 524288
where the time goes:
time: 23.5 us; the launch traced here: 23.4 us
  Pallas kernels  22.7 us (97%)
  local copies, waits for them, and re-layouts  0.71 us (3%)
    pallas_call x1, Pallas kernels, fused(): pl.pallas_call(partial(fused_kernel, dims), out_shape=pltpu.VMEM((tokens,...  22.7 us
    unnamed x1, local copies, waits for them, and re-layouts  0.71 us

commit v1 on v0

v1 whole, which is shorter than its diff:
```python
import math
from functools import partial, reduce

import jax
import jax.numpy as jnp
import numpy as np
from jax import lax
from jax.experimental import pallas as pl
from jax.experimental.pallas import tpu as pltpu
from jax.sharding import PartitionSpec as P

HEADS = 16


FLOOR_SCORE = -1e30


def divisor_block(length, limit):
    extent = min(length, limit)
    while length % extent:
        extent -= 1
    return extent


def fresh_state(count, rows, width):
    return (
        jnp.full((count, rows), FLOOR_SCORE, jnp.float32),
        jnp.zeros((count, rows), jnp.float32),
        jnp.zeros((count, rows, width), jnp.float32),
    )


def finish_state(state):
    row_max, denominator, summed = state
    return (summed / denominator[..., None], row_max + jnp.log(denominator))


def online_step(state, query_rows, query_rank, key_rows, value_rows, key_rank):
    row_max, denominator, summed = state
    scale = query_rows.shape[-1] ** (-0.5)
    scores = (
        jnp.einsum("inh,ibh->inb", query_rows, key_rows, preferred_element_type=jnp.float32) * scale
    )
    scores = jnp.where(key_rank[None, None, :] <= query_rank[None, :, None], scores, FLOOR_SCORE)
    new_max = jnp.maximum(row_max, jnp.max(scores, axis=2))
    weights = jnp.exp(scores - new_max[..., None])
    rescale = jnp.exp(row_max - new_max)
    denominator = denominator * rescale + jnp.sum(weights, axis=2)
    summed = summed * rescale[..., None] + jnp.einsum(
        "inb,ibh->inh", weights.astype(jnp.bfloat16), value_rows, preferred_element_type=jnp.float32
    )
    return (new_max, denominator, summed)


def attend_keys(state, query_rows, query_rank, key_rows, value_rows, key_rank, stop=None):
    length = key_rows.shape[1]
    block = divisor_block(length, 512)

    def advance(index, carry):
        start = index * block
        piece_keys = lax.dynamic_slice_in_dim(key_rows, start, block, 1)
        piece_values = lax.dynamic_slice_in_dim(value_rows, start, block, 1)
        piece_rank = lax.dynamic_slice_in_dim(key_rank, start, block, 0)
        return online_step(carry, query_rows, query_rank, piece_keys, piece_values, piece_rank)

    upper = length // block if stop is None else stop
    return lax.fori_loop(0, upper, advance, state)


def attend(query_rows, query_rank, key_rows, value_rows, key_rank):
    count, length, width = query_rows.shape
    block = divisor_block(length, 512)
    steps = length // block
    query_split = query_rows.reshape(count, steps, block, width).swapaxes(0, 1)
    rank_split = query_rank.reshape(steps, block)

    def one_block(pieces):
        state = attend_keys(
            fresh_state(count, block, width),
            pieces[0],
            pieces[1],
            key_rows,
            value_rows,
            key_rank,
            pieces[2] + 1,
        )
        return finish_state(state)

    outputs, lses = lax.map(
        one_block, (query_split, rank_split, jnp.arange(steps, dtype=jnp.int32))
    )
    return (
        outputs.swapaxes(0, 1).reshape(count, length, width),
        lses.swapaxes(0, 1).reshape(count, length),
    )


def merge_levels(parts):
    row_max = reduce(jnp.maximum, [lse for _, lse in parts])
    weights = [jnp.exp(lse - row_max) for _, lse in parts]
    denominator = reduce(jnp.add, weights)
    summed = reduce(
        jnp.add, [weight[..., None] * output for weight, (output, _) in zip(weights, parts)]
    )
    return (summed / denominator[..., None], row_max + jnp.log(denominator))


def on_device(queries, key_rows, value_rows):
    tokens, features = queries.shape
    heads = HEADS
    width = features // heads
    outer_count = lax.axis_size("outer")
    inner_count = lax.axis_size("inner")
    outer_index = lax.axis_index("outer")
    inner_index = lax.axis_index("inner")
    per_device = 4 * heads // inner_count
    quarter = tokens // 4
    sixteenth = tokens // 16
    class_len = quarter * inner_count
    far_len = sixteenth * inner_count

    def to_items(array):
        return (
            array.reshape(quarter, 4, heads, width)
            .transpose(2, 1, 0, 3)
            .reshape(4 * heads, quarter, width)
        )

    local_ranks = jnp.arange(tokens, dtype=jnp.int32)
    head_major = [
        a.reshape(tokens, heads, width).transpose(1, 0, 2) for a in (queries, key_rows, value_rows)
    ]
    near_out, near_lse = attend(
        head_major[0], local_ranks, head_major[1], head_major[2], local_ranks
    )
    near_out = near_out.transpose(1, 0, 2)
    near_lse = near_lse.T
    item_index = inner_index * per_device + jnp.arange(per_device, dtype=jnp.int32)
    band = item_index // 16
    far_query_rank = outer_index * far_len + jnp.arange(far_len, dtype=jnp.int32)
    pick = np.array(
        [head * 16 + head // 4 * 4 + residue for head in range(heads) for residue in range(4)],
        np.int32,
    )

    def to_sixteen(array):
        spread = (
            array.reshape(sixteenth, 16, heads, width)
            .transpose(2, 1, 0, 3)
            .reshape(16 * heads, sixteenth, width)
        )
        return jnp.take(spread, pick, axis=0)

    gathered_k, gathered_v = (
        lax.all_gather(to_sixteen(key_rows), "outer", axis=1, tiled=True),
        lax.all_gather(to_sixteen(value_rows), "outer", axis=1, tiled=True),
    )
    mid_q, mid_k, mid_v, far_k, far_v = (
        lax.all_to_all(to_items(queries), "inner", split_axis=0, concat_axis=1, tiled=True),
        lax.all_to_all(to_items(key_rows), "inner", split_axis=0, concat_axis=1, tiled=True),
        lax.all_to_all(to_items(value_rows), "inner", split_axis=0, concat_axis=1, tiled=True),
        lax.all_to_all(gathered_k, "inner", split_axis=0, concat_axis=1, tiled=True),
        lax.all_to_all(gathered_v, "inner", split_axis=0, concat_axis=1, tiled=True),
    )
    split = mid_q.reshape(per_device, far_len, 4, width)
    picker = jnp.broadcast_to(band[:, None, None, None], (per_device, far_len, 1, width))
    far_q = jnp.take_along_axis(split, picker, axis=2)[:, :, 0, :]
    position = jnp.arange(far_k.shape[1], dtype=jnp.int32)
    far_key_rank = (
        position // sixteenth % outer_count * far_len
        + position // (outer_count * sixteenth) * sixteenth
        + position % sixteenth
    )
    far_state = attend_keys(
        fresh_state(per_device, far_len, width), far_q, far_query_rank, far_k, far_v, far_key_rank
    )
    far_out, far_lse = finish_state(far_state)
    class_ranks = jnp.arange(class_len, dtype=jnp.int32)
    mid_out, mid_lse = attend(mid_q, class_ranks, mid_k, mid_v, class_ranks)
    back_mid, back_mid_lse, back_far, back_far_lse = (
        lax.all_to_all(mid_out, "inner", split_axis=1, concat_axis=0, tiled=True),
        lax.all_to_all(mid_lse, "inner", split_axis=1, concat_axis=0, tiled=True),
        lax.all_to_all(far_out, "inner", split_axis=1, concat_axis=0, tiled=True),
        lax.all_to_all(far_lse, "inner", split_axis=1, concat_axis=0, tiled=True),
    )
    selector = np.array(
        [[band_index == head // 4 for band_index in range(4)] for head in range(heads)]
    )
    spread_out = jnp.where(
        selector[:, :, None, None, None], back_far.reshape(heads, 1, 4, sixteenth, width), 0.0
    )
    spread_lse = jnp.where(
        selector[:, :, None, None], back_far_lse.reshape(heads, 1, 4, sixteenth), FLOOR_SCORE
    )
    far_placed = (
        spread_out.reshape(heads, 16, sixteenth, width)
        .transpose(2, 1, 0, 3)
        .reshape(tokens, heads, width)
    )
    far_placed_lse = (
        spread_lse.reshape(heads, 16, sixteenth).transpose(2, 1, 0).reshape(tokens, heads)
    )
    placed = (
        back_mid.reshape(heads, 4, quarter, width)
        .transpose(2, 1, 0, 3)
        .reshape(tokens, heads, width)
    )
    placed_lse = back_mid_lse.reshape(heads, 4, quarter).transpose(2, 1, 0).reshape(tokens, heads)
    combined, _ = merge_levels(
        [(near_out, near_lse), (placed, placed_lse), (far_placed, far_placed_lse)]
    )
    return combined.reshape(tokens, features)


def fused_kernel(
    dims, q_ref, k_ref, v_ref, out_ref, q_held, k_held, v_held, q_rows, k_rows, v_rows, q_buf, k_buf, v_buf, far_k, far_v,
    top_ref, total_ref, sum_ref, ready, ready_half, landed,
    spare, send_sem, in_sem, far_sem, back_sem, held_sem, stage_sem,
):
    inner, outer, tokens, slab, width = dims
    chips = inner // 2
    half = inner // 2
    pairs = half // 2
    run = tokens // 16
    tile = tokens // 4
    wide = slab * inner // 4
    me = lax.axis_index("inner")
    mine = lax.axis_index("outer")
    chip = me // 2
    core = lax.rem(me, 2)
    side = me // half
    band = me * 4 // inner
    mesh_id = pl.DeviceIdType.MESH
    sources = (k_ref, v_ref, q_ref)
    held = (k_held, v_held, q_held)
    placed = (k_rows, v_rows, q_rows)
    buffers = (k_buf, v_buf, q_buf)
    pick_k, pick_v, rest_k, rest_v, whole_q = range(5)
    pieces = (
        (0, 0, tile),
        (1, 0, tile),
        (0, tile, tokens),
        (1, tile, tokens),
        (2, 0, tokens),
    )

    def columns(index):
        return pl.ds(pl.multiple_of(index * slab, slab), slab)

    def category(which, peer, owner):
        apart = owner // half != peer // half
        late = 4 + owner % half // 2
        if which < 2:
            return jnp.where(apart, 2, 0)
        early = peer // half == (0 if which == whole_q else 1)
        return jnp.where(apart, jnp.where(early, 3, late), 1)

    def drain(semaphore, rows):
        place = spare.at[0 : rows // 2]
        pltpu.make_async_copy(place, place, semaphore).wait()

    def inbound(which, peer, owner):
        array, start, stop = pieces[which]
        return pltpu.make_async_remote_copy(
            src_ref=placed[array].at[start:stop, columns(peer)],
            dst_ref=buffers[array].at[owner, start:stop, :],
            send_sem=send_sem.at[0],
            recv_sem=in_sem.at[category(which, peer, owner)],
            device_id={"inner": peer},
            device_id_type=mesh_id,
        )

    def farbound(which, part, peer, owner):
        blocks = pl.ds(part * half, half)
        return pltpu.make_async_remote_copy(
            src_ref=buffers[which].at[blocks, 0:tile, :],
            dst_ref=(far_k, far_v)[which].at[owner, blocks],
            send_sem=send_sem.at[1],
            recv_sem=far_sem.at[owner],
            device_id={"outer": peer},
            device_id_type=mesh_id,
        )

    def backbound(peer, owner):
        return pltpu.make_async_remote_copy(
            src_ref=ready.at[peer],
            dst_ref=out_ref.at[:, columns(owner)],
            send_sem=send_sem.at[2],
            recv_sem=back_sem.at[0],
            device_id={"inner": peer},
            device_id_type=mesh_id,
        )

    def crossbound(peer, owner):
        return pltpu.make_async_remote_copy(
            src_ref=ready_half.at[peer],
            dst_ref=landed.at[:, columns(owner)],
            send_sem=send_sem.at[2],
            recv_sem=back_sem.at[1 + owner % half // 2],
            device_id={"inner": peer},
            device_id_type=mesh_id,
        )

    own_held = [
        pltpu.make_async_copy(sources[which], held[which], held_sem.at[which]) for which in range(3)
    ]
    for copy in own_held:
        copy.start()

    barrier = pltpu.get_barrier_semaphore()
    partner = chip * 2 + 1 - core

    def greet(place):
        pl.semaphore_signal(barrier, inc=1, device_id=place, device_id_type=mesh_id)

    greet({"inner": partner})
    for step in range(1, outer):
        greet({"inner": chip * 2 + 1, "outer": lax.rem(mine + step, outer)})
    for other in range(chips):
        gap = jnp.abs(chip - other)
        counter = 0 if other >= chips // 2 else jnp.where(gap > 1, 1, 0)

        @pl.when(gap > 0)
        def _():
            greet({"inner": other * 2 + counter})

    def row_place(shape, axis, first):
        row = lax.broadcasted_iota(jnp.int32, shape, axis)
        residue = 4 * lax.rem(first + row // tile, 4) + row % tile // run
        return row % run * 16 + residue

    square = (tokens, tokens)
    at_row = lax.broadcasted_iota(jnp.int32, square, 0)
    at_column = lax.broadcasted_iota(jnp.int32, square, 1)
    for which in range(3):
        own_held[which].wait()
        for first in range(4):
            place = slice(first * wide, (first + 1) * wide)
            order = (row_place(square, 0, first) == at_column).astype(jnp.float32)
            placed[which][:, place] = jnp.dot(
                order.astype(jnp.bfloat16), held[which][:, place], preferred_element_type=jnp.float32
            ).astype(jnp.bfloat16)

    for other in range(outer - 1):

        @pl.when(mine <= other)
        def _():
            far_k[other] = jnp.zeros((inner, tile, slab), jnp.bfloat16)
            far_v[other] = jnp.zeros((inner, tile, slab), jnp.bfloat16)

    for which in range(3):
        buffers[which][me] = placed[which][:, columns(me)]

    adjacent = jnp.where(chip == 0, 1, 2)
    near_count = 1 + 2 * jnp.where(side == 0, adjacent, chips - 1)
    rest_count = 1 + 2 * (outer - 1) + jnp.where(side == 0, 2 * (chips - 1 - adjacent), 0)

    def pass_on(first, stage, count):
        @pl.when(core == first)
        def _():
            pl.semaphore_wait(barrier, count)
            pl.semaphore_signal(
                stage_sem.at[stage], inc=1, device_id={"inner": partner}, device_id_type=mesh_id
            )

        @pl.when(core != first)
        def _():
            pl.semaphore_wait(stage_sem.at[stage], 1)

    def send(which, distance):
        for other in range(2):

            @pl.when(chip + distance < chips)
            def _():
                inbound(which, (chip + distance) * 2 + other, me).start()

            @pl.when(chip - distance >= 0)
            def _():
                inbound(which, (chip - distance) * 2 + other, me).start()

    picks = (pick_k, pick_v)
    rest = (rest_k, rest_v)
    pass_on(0, 0, near_count)
    for which in range(5):
        inbound(which, partner, me).start()

    @pl.when(side == 0)
    def _():
        for which in picks:
            send(which, 1)
        for which in rest:
            send(which, 1)

        @pl.when(chip == 0)
        def _():
            send(whole_q, 1)

        pass_on(1, 1, rest_count)
        for distance in range(chips - 1, 1, -1):
            for which in picks:
                send(which, distance)
        for distance in range(chips - 1, 1, -1):
            for which in rest:
                send(which, distance)
        for distance in range(chips - 1, 1, -1):
            send(whole_q, distance)

        @pl.when(chip > 0)
        def _():
            send(whole_q, 1)

    @pl.when(side == 1)
    def _():
        for distance in range(chips - 1, 0, -1):
            for which in picks:
                send(which, distance)
        for distance in range(chips - 1, 0, -1):
            send(whole_q, distance)
        for which in rest:
            send(which, 1)
        for distance in range(chips - 1, 1, -1):
            for which in rest:
                send(which, distance)

    def forward(part):
        for which in range(2):
            for other in range(1, outer):

                @pl.when(mine < other)
                def _():
                    farbound(which, part, other, mine).start()

    same = at_row % tile // run == at_column % tile // run
    both = (at_row < tile) & (at_column < tile)
    below = jnp.where(same, jnp.where(both, 1.0, 0.0), FLOOR_SCORE)
    before = row_place(square, 1, band) <= row_place(square, 0, band)
    diagonal = jnp.where(
        before, jnp.where(same, jnp.where(both, math.log2(3.0), 1.0), 0.0), FLOOR_SCORE
    )
    never = jnp.full(square, FLOOR_SCORE, jnp.float32)

    def twice(table):
        return jnp.concatenate([table, table], axis=0)

    below_pair = twice(jnp.concatenate([below, below], axis=1))
    below_pair = jnp.concatenate([below_pair, below_pair], axis=0)
    edge_pair = jnp.concatenate(
        [jnp.concatenate([diagonal, never], axis=1), jnp.concatenate([below, diagonal], axis=1)], axis=0
    )
    edge_pair = twice(edge_pair)
    far_rows = inner * tile
    far_shape = (pairs * 4 * tile, (outer - 1) * far_rows)
    far_query = lax.broadcasted_iota(jnp.int32, far_shape, 0)
    far_key = lax.broadcasted_iota(jnp.int32, far_shape, 1)
    far_table = jnp.where(
        (far_query % tile // run == far_key % tile // run) & (far_key // far_rows < mine), 0.0, FLOOR_SCORE
    )
    factor = width ** (-0.5) * math.log2(math.e)
    contract = (((1,), (1,)), ((), ()))

    def by_head(rows):
        lane_head = lax.broadcasted_iota(jnp.int32, rows.shape, 1) // width
        return jnp.concatenate(
            [jnp.where(lane_head == head, rows, jnp.zeros_like(rows)) for head in range(2)], axis=0
        )

    def attend_block(old, rows, keys, values, table):
        scores = lax.dot_general(rows, keys, contract, preferred_element_type=jnp.float32)
        scores = scores * factor + table
        top = jnp.max(scores, axis=1, keepdims=True)
        if old is not None:
            top = jnp.maximum(top, old[0])
        weights = jnp.exp2(scores - top)
        total = jnp.sum(weights, axis=1, keepdims=True)
        summed = jnp.dot(weights.astype(jnp.bfloat16), values, preferred_element_type=jnp.float32)
        if old is not None:
            rescale = jnp.exp2(old[0] - top)
            total = total + old[1] * rescale
            summed = summed + old[2] * rescale
        return top, total, summed

    def load_state(index, pair):
        return (
            top_ref[index, pair].reshape(4 * tokens, 1),
            total_ref[index, pair].reshape(4 * tokens, 1),
            sum_ref[index, pair].reshape(4 * tokens, slab),
        )

    def keep_state(index, pair, state):
        top_ref[index, pair] = state[0].reshape(4, tokens, 1)
        total_ref[index, pair] = state[1].reshape(4, tokens, 1)
        sum_ref[index, pair] = state[2].reshape(4, tokens, slab)

    def pair_queries(index, pair):
        rows = q_buf[pl.ds(index * half + 2 * pair, 2)].reshape(2 * tokens, slab)
        return by_head(rows)

    def edge(index, pair, old):
        blocks = pl.ds(index * half, 2 * pair + 2)
        count = (2 * pair + 2) * tokens
        keys = k_buf[blocks].reshape(count, slab)
        values = v_buf[blocks].reshape(count, slab)
        table = jnp.concatenate([below_pair] * pair + [edge_pair], axis=1)
        return attend_block(old, pair_queries(index, pair), keys, values, table)

    def far_block(index):
        rows = [
            by_head(q_buf[pl.ds(index * half + 2 * pair, 2), 0:tile].reshape(2 * tile, slab))
            for pair in range(pairs)
        ]
        count = pairs * 4 * tile
        old = (
            top_ref[index, :, :, 0:tile].reshape(count, 1),
            total_ref[index, :, :, 0:tile].reshape(count, 1),
            sum_ref[index, :, :, 0:tile].reshape(count, slab),
        )
        keys = far_k[...].reshape((outer - 1) * far_rows, slab)
        values = far_v[...].reshape((outer - 1) * far_rows, slab)
        top, total, summed = attend_block(old, jnp.concatenate(rows, axis=0), keys, values, far_table)
        top_ref[index, :, :, 0:tile] = top.reshape(pairs, 4, tile, 1)
        total_ref[index, :, :, 0:tile] = total.reshape(pairs, 4, tile, 1)
        sum_ref[index, :, :, 0:tile] = summed.reshape(pairs, 4, tile, slab)

    pair_rows = (2 * tokens, 2 * tokens)
    natural = lax.broadcasted_iota(jnp.int32, pair_rows, 0)
    stored = lax.broadcasted_iota(jnp.int32, pair_rows, 1)
    stored_place = stored // tokens * tokens + row_place(pair_rows, 1, band) % tokens
    restore = (natural == stored_place).astype(jnp.float32).astype(jnp.bfloat16)
    lane_head = lax.broadcasted_iota(jnp.int32, (2 * tokens, slab), 1) // width

    def finish(index, pair):
        summed = sum_ref[index, pair] / total_ref[index, pair]
        summed = summed.reshape(2, 2 * tokens, slab)
        return jnp.where(lane_head == 0, summed[0], summed[1])

    def restored(result, exact):
        coarse = result.astype(jnp.bfloat16)
        moved = jnp.dot(restore, coarse, preferred_element_type=jnp.float32)
        if exact:
            rest = (result - coarse.astype(jnp.float32)).astype(jnp.bfloat16)
            moved = moved + jnp.dot(restore, rest, preferred_element_type=jnp.float32)
        return moved.reshape(2, tokens, slab)

    here = side * half
    there = (1 - side) * half
    drain(in_sem.at[0], (half - 1) * 2 * tile)

    @pl.when(side == 1)
    def _():
        pass_on(1, 1, rest_count)

    forward(side)
    drain(in_sem.at[1], (half - 1) * (3 * tokens - 2 * tile))
    for pair in range(pairs):
        keep_state(side, pair, edge(side, pair, None))
        other_count = 4 * tokens
        keep_state(
            1 - side,
            pair,
            (
                jnp.full((other_count, 1), FLOOR_SCORE, jnp.float32),
                jnp.zeros((other_count, 1), jnp.float32),
                jnp.zeros((other_count, slab), jnp.float32),
            ),
        )
    drain(in_sem.at[2], half * 2 * tile)
    forward(1 - side)

    @pl.when(side == 0)
    def _():
        drain(in_sem.at[3], half * tokens)

    @pl.when(side == 1)
    def _():
        drain(in_sem.at[3], half * 2 * (tokens - tile))

    low_keys = k_buf[0:half].reshape(half * tokens, slab)
    low_values = v_buf[0:half].reshape(half * tokens, slab)
    for pair in range(pairs):
        table = jnp.concatenate([below_pair] * pairs, axis=1)
        keep_state(
            1,
            pair,
            attend_block(load_state(1, pair), pair_queries(1, pair), low_keys, low_values, table),
        )

    for other in range(outer - 1):

        @pl.when(mine > other)
        def _():
            drain(far_sem.at[other], 2 * far_rows)

    far_block(side)
    for pair in range(pairs):
        moved = restored(finish(side, pair), True)
        for step in range(2):
            peer = here + 2 * pair + step
            ready[peer] = moved[step]

            @pl.when(peer == me)
            def _():
                out_ref[:, columns(me)] = moved[step]

            @pl.when(peer != me)
            def _():
                backbound(peer, me).start()

    for pair in range(pairs):

        @pl.when(side == 0)
        def _():
            drain(in_sem.at[4 + pair], 4 * (tokens - tile))

        @pl.when(side == 1)
        def _():
            drain(in_sem.at[4 + pair], 2 * tokens)

        keep_state(1 - side, pair, edge(1 - side, pair, load_state(1 - side, pair)))
        if pair == pairs - 1:
            far_block(1 - side)
    for pair in range(pairs):
        moved = restored(finish(1 - side, pair), False).astype(jnp.bfloat16)
        for step in range(2):
            peer = there + 2 * pair + step
            ready_half[peer] = moved[step]
            crossbound(peer, me).start()

    drain(back_sem.at[0], (half - 1) * 2 * tokens)
    for pair in range(pairs):
        drain(back_sem.at[1 + pair], 2 * tokens)
        for step in (2 * pair, 2 * pair + 1):
            owner = there + step
            out_ref[:, columns(owner)] = landed[:, columns(owner)].astype(jnp.float32)

    drain(send_sem.at[0], (inner - 1) * 3 * tokens)
    drain(send_sem.at[2], (half - 1) * 2 * tokens + half * tokens)
    for count in range(1, outer):

        @pl.when(outer - 1 - mine == count)
        def _():
            drain(send_sem.at[1], count * 2 * far_rows)


def fused(queries, key_rows, value_rows):
    tokens, features = queries.shape
    inner = lax.axis_size("inner")
    outer = lax.axis_size("outer")
    slab = features // inner
    tile = tokens // 4
    pairs = inner // 4
    any_space = pl.BlockSpec(memory_space=pl.ANY)
    dims = (inner, outer, tokens, slab, features // HEADS)
    return pl.pallas_call(
        partial(fused_kernel, dims),
        out_shape=pltpu.VMEM((tokens, features), jnp.float32),
        in_specs=[any_space] * 3,
        out_specs=pl.BlockSpec(memory_space=pltpu.VMEM),
        scratch_shapes=[
            *[pltpu.VMEM((tokens, features), jnp.bfloat16)] * 6,
            *[pltpu.VMEM((inner, tokens, slab), jnp.bfloat16)] * 3,
            *[pltpu.VMEM((outer - 1, inner, tile, slab), jnp.bfloat16)] * 2,
            *[pltpu.VMEM((2, pairs, 4, tokens, 1), jnp.float32)] * 2,
            pltpu.VMEM((2, pairs, 4, tokens, slab), jnp.float32),
            pltpu.VMEM((inner, tokens, slab), jnp.float32),
            pltpu.VMEM((inner, tokens, slab), jnp.bfloat16),
            pltpu.VMEM((tokens, features), jnp.bfloat16),
            pltpu.VMEM((inner * 2 * tokens, slab), jnp.float32),
            pltpu.SemaphoreType.DMA((3,)),
            pltpu.SemaphoreType.DMA((4 + pairs,)),
            pltpu.SemaphoreType.DMA((outer - 1,)),
            pltpu.SemaphoreType.DMA((1 + pairs,)),
            pltpu.SemaphoreType.DMA((3,)),
            pltpu.SemaphoreType.REGULAR((2,)),
        ],
        compiler_params=pltpu.CompilerParams(collective_id=0, has_side_effects=True),
    )(queries, key_rows, value_rows)


def device_program(queries, key_rows, value_rows):
    tokens, features = queries.shape
    inner = lax.axis_size("inner")
    outer = lax.axis_size("outer")
    width = features // HEADS
    fits = (
        inner * 2 == HEADS
        and outer > 1
        and inner % 4 == 0
        and width * 2 == 128
        and tokens % 64 == 0
        and inner * tokens <= 1024
        and (outer - 1) * inner * tokens // 4 <= 1024
    )
    if fits:
        return fused(queries, key_rows, value_rows)
    return on_device(queries, key_rows, value_rows)


def solution(mesh):
    placed = (P(("outer", "inner"), None), P(("outer", "inner"), None), P(("outer", "inner"), None))
    return jax.shard_map(
        device_program,
        mesh=mesh,
        in_specs=placed,
        out_specs=P(("outer", "inner"), None),
        check_vma=False,
    )
```

time: 23.5 us -> 21.8 us (0.928)
  the two profiles are of different devices: /device:TPU:0 before, /device:TPU:5 now
where the time goes in v1:
time: 21.8 us; the launch traced here: 21.7 us
  Pallas kernels  21 us (96%)
  local copies, waits for them, and re-layouts  0.71 us (3%)
    pallas_call x1, Pallas kernels, fused(): pl.pallas_call(partial(fused_kernel, dims), out_shape=pltpu.VMEM((tokens,...  21 us
    unnamed x1, local copies, waits for them, and re-layouts  0.71 us

profile of v1, /device:TPU:5, one launch (start us, length us, event | category | flops | bytes accessed | tf_op | source)
XLA Modules:
  0.0 21.7 jit_solution(13425503633508890274)
XLA Ops:
  0.0 21.0 %shard_map.37 = f32[64,1024]{1,0:T(8,128)S(1)} custom-call(bf16[64,1024]{1,0:T(8,128)(2,1)} %q_ref.1, bf16[64,1024]{1,0:T(8,128)(2,1)} %k_ref.1, bf16[64,1024]{1,0:T(8,128)(2,1)} %v_ref.1), custom_call_target="tpu_custom_call" | custom-call | tf_op jit(solution)/shard_map/pallas_call | solution.py:653
  21.0 0.7 %copy.5 = f32[64,1024]{1,0:T(8,128)} copy(f32[64,1024]{1,0:T(8,128)S(1)} %shard_map.37) | data formatting | bytes 524288

commit v2 on v1

--- a/solution.py
+++ b/solution.py
@@ -214,7 +214,7 @@
 
 def fused_kernel(
     dims, q_ref, k_ref, v_ref, out_ref, q_held, k_held, v_held, q_rows, k_rows, v_rows, q_buf, k_buf, v_buf, far_k, far_v,
-    top_ref, total_ref, sum_ref, ready, ready_half, landed,
+    state_ref, ready, ready_half, landed,
     spare, send_sem, in_sem, far_sem, back_sem, held_sem, stage_sem,
 ):
     inner, outer, tokens, slab, width = dims
@@ -247,25 +247,17 @@
     def columns(index):
         return pl.ds(pl.multiple_of(index * slab, slab), slab)
 
-    def category(which, peer, owner):
-        apart = owner // half != peer // half
-        late = 4 + owner % half // 2
-        if which < 2:
-            return jnp.where(apart, 2, 0)
-        early = peer // half == (0 if which == whole_q else 1)
-        return jnp.where(apart, jnp.where(early, 3, late), 1)
-
     def drain(semaphore, rows):
         place = spare.at[0 : rows // 2]
         pltpu.make_async_copy(place, place, semaphore).wait()
 
-    def inbound(which, peer, owner):
+    def inbound(which, peer, owner, arrival):
         array, start, stop = pieces[which]
         return pltpu.make_async_remote_copy(
             src_ref=placed[array].at[start:stop, columns(peer)],
             dst_ref=buffers[array].at[owner, start:stop, :],
             send_sem=send_sem.at[0],
-            recv_sem=in_sem.at[category(which, peer, owner)],
+            recv_sem=in_sem.at[arrival],
             device_id={"inner": peer},
             device_id_type=mesh_id,
         )
@@ -317,10 +309,12 @@
     for step in range(1, outer):
         greet({"inner": chip * 2 + 1, "outer": lax.rem(mine + step, outer)})
     for other in range(chips):
-        gap = jnp.abs(chip - other)
-        counter = 0 if other >= chips // 2 else jnp.where(gap > 1, 1, 0)
-
-        @pl.when(gap > 0)
+        if other < chips // 2:
+            counter = jnp.where(jnp.abs(chip - other) > 1, 1, 0)
+        else:
+            counter = jnp.where(chip > other, 1, 0)
+
+        @pl.when(chip != other)
         def _():
             greet({"inner": other * 2 + counter})
 
@@ -332,28 +326,23 @@
     square = (tokens, tokens)
     at_row = lax.broadcasted_iota(jnp.int32, square, 0)
     at_column = lax.broadcasted_iota(jnp.int32, square, 1)
-    for which in range(3):
+    orders = [
+        (row_place(square, 0, first) == at_column).astype(jnp.float32).astype(jnp.bfloat16)
+        for first in range(4)
+    ]
+
+    def place_rows(which):
         own_held[which].wait()
         for first in range(4):
             place = slice(first * wide, (first + 1) * wide)
-            order = (row_place(square, 0, first) == at_column).astype(jnp.float32)
             placed[which][:, place] = jnp.dot(
-                order.astype(jnp.bfloat16), held[which][:, place], preferred_element_type=jnp.float32
+                orders[first], held[which][:, place], preferred_element_type=jnp.float32
             ).astype(jnp.bfloat16)
-
-    for other in range(outer - 1):
-
-        @pl.when(mine <= other)
-        def _():
-            far_k[other] = jnp.zeros((inner, tile, slab), jnp.bfloat16)
-            far_v[other] = jnp.zeros((inner, tile, slab), jnp.bfloat16)
-
-    for which in range(3):
         buffers[which][me] = placed[which][:, columns(me)]
 
     adjacent = jnp.where(chip == 0, 1, 2)
-    near_count = 1 + 2 * jnp.where(side == 0, adjacent, chips - 1)
-    rest_count = 1 + 2 * (outer - 1) + jnp.where(side == 0, 2 * (chips - 1 - adjacent), 0)
+    near_count = 1 + 2 * jnp.where(side == 0, adjacent, chip)
+    rest_count = 1 + 2 * (outer - 1) + 2 * (chips - 1 - jnp.where(side == 0, adjacent, chip))
 
     def pass_on(first, stage, count):
         @pl.when(core == first)
@@ -367,60 +356,84 @@
         def _():
             pl.semaphore_wait(stage_sem.at[stage], 1)
 
-    def send(which, distance):
-        for other in range(2):
-
-            @pl.when(chip + distance < chips)
-            def _():
-                inbound(which, (chip + distance) * 2 + other, me).start()
-
-            @pl.when(chip - distance >= 0)
-            def _():
-                inbound(which, (chip - distance) * 2 + other, me).start()
-
     picks = (pick_k, pick_v)
     rest = (rest_k, rest_v)
+    query = (whole_q,)
+
+    def arrival_of(which, source, target):
+        low = chips // 2
+        apart = (source < low) != (target < low)
+        if which in picks:
+            return 2 if apart else 0
+        if not apart:
+            return 1
+        early = (which == whole_q) == (target < low)
+        return 3 if early else 4 + source % low
+
+    def send(source, batches):
+        for group, targets in batches:
+            for target in targets:
+                for which in group:
+                    for other in range(2):
+                        arrival = arrival_of(which, source, target)
+                        inbound(which, target * 2 + other, me, arrival).start()
+
+    def send_partner(group):
+        for which in group:
+            inbound(which, partner, me, 0 if which in picks else 1).start()
+
+    place_rows(0)
+    place_rows(1)
     pass_on(0, 0, near_count)
-    for which in range(5):
-        inbound(which, partner, me).start()
-
-    @pl.when(side == 0)
-    def _():
-        for which in picks:
-            send(which, 1)
-        for which in rest:
-            send(which, 1)
-
-        @pl.when(chip == 0)
+    send_partner(picks + rest)
+
+    @pl.when(chip == 0)
+    def _():
+        send(0, ((picks, (1,)), (rest, (1,))))
+
+    @pl.when(chip == 1)
+    def _():
+        send(1, ((picks, (2, 0)), (rest, (2, 0))))
+
+    @pl.when(chip == 2)
+    def _():
+        send(2, ((picks, (0, 1)),))
+
+    @pl.when(chip == 3)
+    def _():
+        send(3, ((picks, (0, 1, 2)),))
+
+    place_rows(2)
+    send_partner(query)
+
+    @pl.when(chip == 0)
+    def _():
+        send(0, ((query, (1,)),))
+        pass_on(1, 1, rest_count)
+        send(0, ((picks, (3, 2)), (rest, (3, 2)), (query, (3, 2))))
+
+    @pl.when(chip == 1)
+    def _():
+        send(1, ((query, (0,)),))
+        pass_on(1, 1, rest_count)
+        send(1, ((picks, (3,)), (rest, (3,)), (query, (3, 2))))
+
+    @pl.when(chip == 2)
+    def _():
+        send(2, ((query, (0, 1)),))
+        pass_on(1, 1, rest_count)
+        send(2, ((picks, (3,)), (rest, (0, 1)), (query, (3,)), (rest, (3,))))
+
+    @pl.when(chip == 3)
+    def _():
+        send(3, ((query, (0, 1, 2)), (rest, (2,)), (rest, (0, 1))))
+
+    for other in range(outer - 1):
+
+        @pl.when(mine <= other)
         def _():
-            send(whole_q, 1)
-
-        pass_on(1, 1, rest_count)
-        for distance in range(chips - 1, 1, -1):
-            for which in picks:
-                send(which, distance)
-        for distance in range(chips - 1, 1, -1):
-            for which in rest:
-                send(which, distance)
-        for distance in range(chips - 1, 1, -1):
-            send(whole_q, distance)
-
-        @pl.when(chip > 0)
-        def _():
-            send(whole_q, 1)
-
-    @pl.when(side == 1)
-    def _():
-        for distance in range(chips - 1, 0, -1):
-            for which in picks:
-                send(which, distance)
-        for distance in range(chips - 1, 0, -1):
-            send(whole_q, distance)
-        for which in rest:
-            send(which, 1)
-        for distance in range(chips - 1, 1, -1):
-            for which in rest:
-                send(which, distance)
+            far_k[other] = jnp.zeros((inner, tile, slab), jnp.bfloat16)
+            far_v[other] = jnp.zeros((inner, tile, slab), jnp.bfloat16)
 
     def forward(part):
         for which in range(2):
@@ -464,62 +477,75 @@
             [jnp.where(lane_head == head, rows, jnp.zeros_like(rows)) for head in range(2)], axis=0
         )
 
-    def attend_block(old, rows, keys, values, table):
+    def across(column):
+        return jnp.broadcast_to(column, (column.shape[0], slab))
+
+    def attend_part(rows, keys, values, table):
         scores = lax.dot_general(rows, keys, contract, preferred_element_type=jnp.float32)
         scores = scores * factor + table
         top = jnp.max(scores, axis=1, keepdims=True)
-        if old is not None:
-            top = jnp.maximum(top, old[0])
         weights = jnp.exp2(scores - top)
         total = jnp.sum(weights, axis=1, keepdims=True)
         summed = jnp.dot(weights.astype(jnp.bfloat16), values, preferred_element_type=jnp.float32)
-        if old is not None:
-            rescale = jnp.exp2(old[0] - top)
-            total = total + old[1] * rescale
-            summed = summed + old[2] * rescale
-        return top, total, summed
+        return across(top), across(total), summed
+
+    def join(one, two):
+        top = jnp.maximum(one[0], two[0])
+        first = jnp.exp2(one[0] - top)
+        second = jnp.exp2(two[0] - top)
+        return top, one[1] * first + two[1] * second, one[2] * first + two[2] * second
+
+    def join_tile(state, far):
+        cut = [part.reshape(4, tokens, slab) for part in state]
+        met = join([part[:, 0:tile] for part in cut], far)
+        return [
+            jnp.concatenate([new, old[:, tile:]], axis=1).reshape(4 * tokens, slab)
+            for new, old in zip(met, cut)
+        ]
 
     def load_state(index, pair):
-        return (
-            top_ref[index, pair].reshape(4 * tokens, 1),
-            total_ref[index, pair].reshape(4 * tokens, 1),
-            sum_ref[index, pair].reshape(4 * tokens, slab),
-        )
+        return [state_ref[which, index, pair] for which in range(3)]
 
     def keep_state(index, pair, state):
-        top_ref[index, pair] = state[0].reshape(4, tokens, 1)
-        total_ref[index, pair] = state[1].reshape(4, tokens, 1)
-        sum_ref[index, pair] = state[2].reshape(4, tokens, slab)
+        for which in range(3):
+            state_ref[which, index, pair] = state[which]
 
     def pair_queries(index, pair):
-        rows = q_buf[pl.ds(index * half + 2 * pair, 2)].reshape(2 * tokens, slab)
-        return by_head(rows)
-
-    def edge(index, pair, old):
-        blocks = pl.ds(index * half, 2 * pair + 2)
-        count = (2 * pair + 2) * tokens
-        keys = k_buf[blocks].reshape(count, slab)
-        values = v_buf[blocks].reshape(count, slab)
+        rows = q_buf[index * half + 2 * pair : index * half + 2 * pair + 2]
+        return by_head(rows.reshape(2 * tokens, slab))
+
+    def span_of(buffer, start, stop):
+        return buffer[start:stop].reshape((stop - start) * tokens, slab)
+
+    def edge(index, pair):
+        start = index * half
+        stop = start + 2 * pair + 2
         table = jnp.concatenate([below_pair] * pair + [edge_pair], axis=1)
-        return attend_block(old, pair_queries(index, pair), keys, values, table)
-
-    def far_block(index):
+        return attend_part(
+            pair_queries(index, pair), span_of(k_buf, start, stop), span_of(v_buf, start, stop), table
+        )
+
+    def below_block(pair):
+        table = jnp.concatenate([below_pair] * pairs, axis=1)
+        return attend_part(
+            pair_queries(1, pair), span_of(k_buf, 0, half), span_of(v_buf, 0, half), table
+        )
+
+    def far_block(index, first, stop):
+        span = stop - first
         rows = [
-            by_head(q_buf[pl.ds(index * half + 2 * pair, 2), 0:tile].reshape(2 * tile, slab))
-            for pair in range(pairs)
+            by_head(
+                q_buf[index * half + 2 * pair : index * half + 2 * pair + 2, 0:tile].reshape(2 * tile, slab)
+            )
+            for pair in range(first, stop)
         ]
-        count = pairs * 4 * tile
-        old = (
-            top_ref[index, :, :, 0:tile].reshape(count, 1),
-            total_ref[index, :, :, 0:tile].reshape(count, 1),
-            sum_ref[index, :, :, 0:tile].reshape(count, slab),
-        )
+        count = span * 4 * tile
         keys = far_k[...].reshape((outer - 1) * far_rows, slab)
         values = far_v[...].reshape((outer - 1) * far_rows, slab)
-        top, total, summed = attend_block(old, jnp.concatenate(rows, axis=0), keys, values, far_table)
-        top_ref[index, :, :, 0:tile] = top.reshape(pairs, 4, tile, 1)
-        total_ref[index, :, :, 0:tile] = total.reshape(pairs, 4, tile, 1)
-        sum_ref[index, :, :, 0:tile] = summed.reshape(pairs, 4, tile, slab)
+        state = attend_part(jnp.concatenate(rows, axis=0), keys, values, far_table[0:count])
+        return [
+            [part.reshape(span, 4, tile, slab)[place] for part in state] for place in range(span)
+        ]
 
     pair_rows = (2 * tokens, 2 * tokens)
     natural = lax.broadcasted_iota(jnp.int32, pair_rows, 0)
@@ -528,9 +554,8 @@
     restore = (natural == stored_place).astype(jnp.float32).astype(jnp.bfloat16)
     lane_head = lax.broadcasted_iota(jnp.int32, (2 * tokens, slab), 1) // width
 
-    def finish(index, pair):
-        summed = sum_ref[index, pair] / total_ref[index, pair]
-        summed = summed.reshape(2, 2 * tokens, slab)
+    def finish(state):
+        summed = (state[2] / state[1]).reshape(2, 2 * tokens, slab)
         return jnp.where(lane_head == 0, summed[0], summed[1])
 
     def restored(result, exact):
@@ -541,90 +566,79 @@
             moved = moved + jnp.dot(restore, rest, preferred_element_type=jnp.float32)
         return moved.reshape(2, tokens, slab)
 
-    here = side * half
-    there = (1 - side) * half
+    def return_near(index, pair, state):
+        moved = restored(finish(state), True)
+        for step in range(2):
+            peer = index * half + 2 * pair + step
+            ready[peer] = moved[step]
+
+            @pl.when(me == peer)
+            def _():
+                out_ref[:, columns(me)] = moved[step]
+
+            @pl.when(me != peer)
+            def _():
+                backbound(peer, me).start()
+
+    def return_apart(index, pair, state):
+        moved = restored(finish(state), False).astype(jnp.bfloat16)
+        for step in range(2):
+            peer = index * half + 2 * pair + step
+            ready_half[peer] = moved[step]
+            crossbound(peer, me).start()
+
     drain(in_sem.at[0], (half - 1) * 2 * tile)
 
-    @pl.when(side == 1)
+    @pl.when(chip == chips - 1)
     def _():
         pass_on(1, 1, rest_count)
 
     forward(side)
-    drain(in_sem.at[1], (half - 1) * (3 * tokens - 2 * tile))
-    for pair in range(pairs):
-        keep_state(side, pair, edge(side, pair, None))
-        other_count = 4 * tokens
-        keep_state(
-            1 - side,
-            pair,
-            (
-                jnp.full((other_count, 1), FLOOR_SCORE, jnp.float32),
-                jnp.zeros((other_count, 1), jnp.float32),
-                jnp.zeros((other_count, slab), jnp.float32),
-            ),
-        )
     drain(in_sem.at[2], half * 2 * tile)
     forward(1 - side)
+    drain(in_sem.at[1], (half - 1) * (3 * tokens - 2 * tile))
+
+    def wait_far():
+        for other in range(outer - 1):
+
+            @pl.when(mine > other)
+            def _():
+                drain(far_sem.at[other], 2 * far_rows)
 
     @pl.when(side == 0)
     def _():
+        for pair in range(pairs):
+            keep_state(0, pair, edge(0, pair))
         drain(in_sem.at[3], half * tokens)
+        for pair in range(pairs):
+            keep_state(1, pair, below_block(pair))
+        wait_far()
+        near_far = far_block(0, 0, pairs)
+        apart_far = far_block(1, 0, pairs)
+        for pair in range(pairs):
+            keep_state(1, pair, join_tile(load_state(1, pair), apart_far[pair]))
+            return_near(0, pair, join_tile(load_state(0, pair), near_far[pair]))
+        for pair in range(pairs):
+            drain(in_sem.at[4 + pair], 4 * (tokens - tile))
+            return_apart(1, pair, join(load_state(1, pair), edge(1, pair)))
 
     @pl.when(side == 1)
     def _():
+        for pair in range(pairs):
+            keep_state(1, pair, edge(1, pair))
         drain(in_sem.at[3], half * 2 * (tokens - tile))
-
-    low_keys = k_buf[0:half].reshape(half * tokens, slab)
-    low_values = v_buf[0:half].reshape(half * tokens, slab)
-    for pair in range(pairs):
-        table = jnp.concatenate([below_pair] * pairs, axis=1)
-        keep_state(
-            1,
-            pair,
-            attend_block(load_state(1, pair), pair_queries(1, pair), low_keys, low_values, table),
-        )
-
-    for other in range(outer - 1):
-
-        @pl.when(mine > other)
-        def _():
-            drain(far_sem.at[other], 2 * far_rows)
-
-    far_block(side)
-    for pair in range(pairs):
-        moved = restored(finish(side, pair), True)
-        for step in range(2):
-            peer = here + 2 * pair + step
-            ready[peer] = moved[step]
-
-            @pl.when(peer == me)
-            def _():
-                out_ref[:, columns(me)] = moved[step]
-
-            @pl.when(peer != me)
-            def _():
-                backbound(peer, me).start()
-
-    for pair in range(pairs):
-
-        @pl.when(side == 0)
-        def _():
-            drain(in_sem.at[4 + pair], 4 * (tokens - tile))
-
-        @pl.when(side == 1)
-        def _():
+        for pair in range(pairs):
+            keep_state(1, pair, join(load_state(1, pair), below_block(pair)))
+        wait_far()
+        for pair in range(pairs):
             drain(in_sem.at[4 + pair], 2 * tokens)
-
-        keep_state(1 - side, pair, edge(1 - side, pair, load_state(1 - side, pair)))
-        if pair == pairs - 1:
-            far_block(1 - side)
-    for pair in range(pairs):
-        moved = restored(finish(1 - side, pair), False).astype(jnp.bfloat16)
-        for step in range(2):
-            peer = there + 2 * pair + step
-            ready_half[peer] = moved[step]
-            crossbound(peer, me).start()
-
+            apart_far = far_block(0, pair, pair + 1)
+            return_apart(0, pair, join_tile(edge(0, pair), apart_far[0]))
+        near_far = far_block(1, 0, pairs)
+        for pair in range(pairs):
+            return_near(1, pair, join_tile(load_state(1, pair), near_far[pair]))
+
+    there = (1 - side) * half
     drain(back_sem.at[0], (half - 1) * 2 * tokens)
     for pair in range(pairs):
         drain(back_sem.at[1 + pair], 2 * tokens)
@@ -659,8 +673,7 @@
             *[pltpu.VMEM((tokens, features), jnp.bfloat16)] * 6,
             *[pltpu.VMEM((inner, tokens, slab), jnp.bfloat16)] * 3,
             *[pltpu.VMEM((outer - 1, inner, tile, slab), jnp.bfloat16)] * 2,
-            *[pltpu.VMEM((2, pairs, 4, tokens, 1), jnp.float32)] * 2,
-            pltpu.VMEM((2, pairs, 4, tokens, slab), jnp.float32),
+            pltpu.VMEM((3, 2, pairs, 4 * tokens, slab), jnp.float32),
             pltpu.VMEM((inner, tokens, slab), jnp.float32),
             pltpu.VMEM((inner, tokens, slab), jnp.bfloat16),
             pltpu.VMEM((tokens, features), jnp.bfloat16),

time: 21.8 us -> 19.4 us (0.89)
  the two profiles are of different devices: /device:TPU:5 before, /device:TPU:0 now
where the time goes in v2:
time: 19.4 us; the launch traced here: 19.2 us
  Pallas kernels  18.5 us (95%)
  local copies, waits for them, and re-layouts  0.71 us (4%)
    pallas_call x1, Pallas kernels, fused(): pl.pallas_call(partial(fused_kernel, dims), out_shape=pltpu.VMEM((tokens,...  18.5 us
    unnamed x1, local copies, waits for them, and re-layouts  0.71 us

profile of v2, /device:TPU:0, one launch (start us, length us, event | category | flops | bytes accessed | tf_op | source)
XLA Modules:
  0.0 19.2 jit_solution(11626707726651680712)
XLA Ops:
  0.0 18.5 %shard_map.37 = f32[64,1024]{1,0:T(8,128)S(1)} custom-call(bf16[64,1024]{1,0:T(8,128)(2,1)} %q_ref.1, bf16[64,1024]{1,0:T(8,128)(2,1)} %k_ref.1, bf16[64,1024]{1,0:T(8,128)(2,1)} %v_ref.1), custom_call_target="tpu_custom_call" | custom-call | tf_op jit(solution)/shard_map/pallas_call | solution.py:667
  18.5 0.7 %copy.5 = f32[64,1024]{1,0:T(8,128)} copy(f32[64,1024]{1,0:T(8,128)S(1)} %shard_map.37) | data formatting | bytes 524288

commit v3 on v2

--- a/solution.py
+++ b/solution.py
@@ -367,8 +367,11 @@
             return 2 if apart else 0
         if not apart:
             return 1
-        early = (which == whole_q) == (target < low)
-        return 3 if early else 4 + source % low
+        if target < low:
+            return 3 if which == whole_q else 4 + source % low
+        if source == 0:
+            return 4
+        return 5 if which == whole_q else 3
 
     def send(source, batches):
         for group, targets in batches:
@@ -393,7 +396,7 @@
 
     @pl.when(chip == 1)
     def _():
-        send(1, ((picks, (2, 0)), (rest, (2, 0))))
+        send(1, ((picks, (2, 0)), ((rest_k,), (2,)), (rest, (0,))))
 
     @pl.when(chip == 2)
     def _():
@@ -410,13 +413,13 @@
     def _():
         send(0, ((query, (1,)),))
         pass_on(1, 1, rest_count)
-        send(0, ((picks, (3, 2)), (rest, (3, 2)), (query, (3, 2))))
+        send(0, ((picks, (3, 2)), (rest, (3,)), (query, (3,)), (rest, (2,)), (query, (2,))))
 
     @pl.when(chip == 1)
     def _():
         send(1, ((query, (0,)),))
         pass_on(1, 1, rest_count)
-        send(1, ((picks, (3,)), (rest, (3,)), (query, (3, 2))))
+        send(1, ((picks, (3,)), (rest, (3,)), ((rest_v,), (2,)), (query, (3, 2))))
 
     @pl.when(chip == 2)
     def _():
@@ -436,11 +439,11 @@
             far_v[other] = jnp.zeros((inner, tile, slab), jnp.bfloat16)
 
     def forward(part):
-        for which in range(2):
-            for other in range(1, outer):
-
-                @pl.when(mine < other)
-                def _():
+        for other in range(outer - 1, 0, -1):
+
+            @pl.when(mine < other)
+            def _():
+                for which in range(2):
                     farbound(which, part, other, mine).start()
 
     same = at_row % tile // run == at_column % tile // run
@@ -555,8 +558,10 @@
     lane_head = lax.broadcasted_iota(jnp.int32, (2 * tokens, slab), 1) // width
 
     def finish(state):
-        summed = (state[2] / state[1]).reshape(2, 2 * tokens, slab)
-        return jnp.where(lane_head == 0, summed[0], summed[1])
+        total, summed = (part.reshape(2, 2 * tokens, slab) for part in state[1:])
+        return jnp.where(lane_head == 0, summed[0], summed[1]) / jnp.where(
+            lane_head == 0, total[0], total[1]
+        )
 
     def restored(result, exact):
         coarse = result.astype(jnp.bfloat16)
@@ -566,19 +571,14 @@
             moved = moved + jnp.dot(restore, rest, preferred_element_type=jnp.float32)
         return moved.reshape(2, tokens, slab)
 
-    def return_near(index, pair, state):
-        moved = restored(finish(state), True)
-        for step in range(2):
-            peer = index * half + 2 * pair + step
-            ready[peer] = moved[step]
-
-            @pl.when(me == peer)
-            def _():
-                out_ref[:, columns(me)] = moved[step]
-
-            @pl.when(me != peer)
-            def _():
-                backbound(peer, me).start()
+    def return_near(index, states):
+        for pair, state in enumerate(states):
+            moved = restored(finish(state), True)
+            for step in range(2):
+                ready[index * half + 2 * pair + step] = moved[step]
+        for step in range(1, half):
+            backbound(index * half + lax.rem(me + step, half), me).start()
+        out_ref[:, columns(me)] = ready[me]
 
     def return_apart(index, pair, state):
         moved = restored(finish(state), False).astype(jnp.bfloat16)
@@ -617,7 +617,9 @@
         apart_far = far_block(1, 0, pairs)
         for pair in range(pairs):
             keep_state(1, pair, join_tile(load_state(1, pair), apart_far[pair]))
-            return_near(0, pair, join_tile(load_state(0, pair), near_far[pair]))
+        return_near(
+            0, [join_tile(load_state(0, pair), near_far[pair]) for pair in range(pairs)]
+        )
         for pair in range(pairs):
             drain(in_sem.at[4 + pair], 4 * (tokens - tile))
             return_apart(1, pair, join(load_state(1, pair), edge(1, pair)))
@@ -626,17 +628,42 @@
     def _():
         for pair in range(pairs):
             keep_state(1, pair, edge(1, pair))
-        drain(in_sem.at[3], half * 2 * (tokens - tile))
-        for pair in range(pairs):
-            keep_state(1, pair, join(load_state(1, pair), below_block(pair)))
+        def join_below():
+            drain(in_sem.at[3], 4 * (tokens - tile))
+            for pair in range(pairs):
+                keep_state(1, pair, join(load_state(1, pair), below_block(pair)))
+
+        drain(in_sem.at[4], 4 * (tokens - tile) + 2 * tokens)
+
+        first = (mine == 0) | (chip == chips - 1)
+
+        @pl.when(jnp.logical_not(first))
+        def _():
+            join_below()
+
         wait_far()
-        for pair in range(pairs):
-            drain(in_sem.at[4 + pair], 2 * tokens)
-            apart_far = far_block(0, pair, pair + 1)
-            return_apart(0, pair, join_tile(edge(0, pair), apart_far[0]))
-        near_far = far_block(1, 0, pairs)
-        for pair in range(pairs):
-            return_near(1, pair, join_tile(load_state(1, pair), near_far[pair]))
+        return_apart(0, 0, join_tile(edge(0, 0), far_block(0, 0, 1)[0]))
+
+        def near_block():
+            near_far = far_block(1, 0, pairs)
+            return_near(
+                1, [join_tile(load_state(1, pair), near_far[pair]) for pair in range(pairs)]
+            )
+
+        @pl.when(first)
+        def _():
+            join_below()
+
+        @pl.when(chip < chips - 1)
+        def _():
+            near_block()
+
+        drain(in_sem.at[5], 2 * tokens)
+        return_apart(0, 1, join_tile(edge(0, 1), far_block(0, 1, 2)[0]))
+
+        @pl.when(chip == chips - 1)
+        def _():
+            near_block()
 
     there = (1 - side) * half
     drain(back_sem.at[0], (half - 1) * 2 * tokens)

time: 19.4 us -> 18.6 us (0.959)
  the two profiles are of different devices: /device:TPU:0 before, /device:TPU:13 now
where the time goes in v3:
time: 18.6 us; the launch traced here: 18.5 us
  Pallas kernels  17.8 us (96%)
  local copies, waits for them, and re-layouts  0.71 us (4%)
    pallas_call x1, Pallas kernels, fused(): pl.pallas_call(partial(fused_kernel, dims), out_shape=pltpu.VMEM((tokens,...  17.8 us
    unnamed x1, local copies, waits for them, and re-layouts  0.71 us

profile of v3, /device:TPU:13, one launch (start us, length us, event | category | flops | bytes accessed | tf_op | source)
XLA Modules:
  0.0 18.5 jit_solution(2251322708802475552)
XLA Ops:
  0.0 17.8 %shard_map.37 = f32[64,1024]{1,0:T(8,128)S(1)} custom-call(bf16[64,1024]{1,0:T(8,128)(2,1)} %q_ref.1, bf16[64,1024]{1,0:T(8,128)(2,1)} %k_ref.1, bf16[64,1024]{1,0:T(8,128)(2,1)} %v_ref.1), custom_call_target="tpu_custom_call" | custom-call | tf_op jit(solution)/shard_map/pallas_call | solution.py:694
  17.8 0.7 %copy.5 = f32[64,1024]{1,0:T(8,128)} copy(f32[64,1024]{1,0:T(8,128)S(1)} %shard_map.37) | data formatting | bytes 524288

commit v4 on v3

--- a/solution.py
+++ b/solution.py
@@ -214,7 +214,7 @@
 
 def fused_kernel(
     dims, q_ref, k_ref, v_ref, out_ref, q_held, k_held, v_held, q_rows, k_rows, v_rows, q_buf, k_buf, v_buf, far_k, far_v,
-    state_ref, ready, ready_half, landed,
+    state_ref, ready, ready_half, landed, side_k, side_v, local_ref, far_out, far_landed,
     spare, send_sem, in_sem, far_sem, back_sem, held_sem, stage_sem,
 ):
     inner, outer, tokens, slab, width = dims
@@ -235,13 +235,14 @@
     held = (k_held, v_held, q_held)
     placed = (k_rows, v_rows, q_rows)
     buffers = (k_buf, v_buf, q_buf)
-    pick_k, pick_v, rest_k, rest_v, whole_q = range(5)
+    pick_k, pick_v, rest_k, rest_v, whole_q, pick_q = range(6)
     pieces = (
         (0, 0, tile),
         (1, 0, tile),
         (0, tile, tokens),
         (1, tile, tokens),
         (2, 0, tokens),
+        (2, 0, tile),
     )
 
     def columns(index):
@@ -283,12 +284,32 @@
             device_id_type=mesh_id,
         )
 
-    def crossbound(peer, owner):
+    def sidebound(which):
+        return pltpu.make_async_remote_copy(
+            src_ref=placed[which].at[:, half * slab : inner * slab],
+            dst_ref=(side_k, side_v)[which],
+            send_sem=send_sem.at[0],
+            recv_sem=in_sem.at[6],
+            device_id={"inner": 1},
+            device_id_type=mesh_id,
+        )
+
+    def partbound(peer):
+        return pltpu.make_async_remote_copy(
+            src_ref=far_out.at[peer],
+            dst_ref=far_landed.at[:, :, columns(me - half)],
+            send_sem=send_sem.at[2],
+            recv_sem=back_sem.at[1],
+            device_id={"inner": peer},
+            device_id_type=mesh_id,
+        )
+
+    def crossbound(peer, owner, arrival):
         return pltpu.make_async_remote_copy(
             src_ref=ready_half.at[peer],
             dst_ref=landed.at[:, columns(owner)],
             send_sem=send_sem.at[2],
-            recv_sem=back_sem.at[1 + owner % half // 2],
+            recv_sem=back_sem.at[arrival],
             device_id={"inner": peer},
             device_id_type=mesh_id,
         )
@@ -394,6 +415,12 @@
     def _():
         send(0, ((picks, (1,)), (rest, (1,))))
 
+        @pl.when(core == 0)
+        def _():
+            for which in range(2):
+                sidebound(which).start()
+
+
     @pl.when(chip == 1)
     def _():
         send(1, ((picks, (2, 0)), ((rest_k,), (2,)), (rest, (0,))))
@@ -413,7 +440,7 @@
     def _():
         send(0, ((query, (1,)),))
         pass_on(1, 1, rest_count)
-        send(0, ((picks, (3, 2)), (rest, (3,)), (query, (3,)), (rest, (2,)), (query, (2,))))
+        send(0, ((picks, (3, 2)), ((pick_q,) + rest, (3, 2))))
 
     @pl.when(chip == 1)
     def _():
@@ -430,6 +457,11 @@
     @pl.when(chip == 3)
     def _():
         send(3, ((query, (0, 1, 2)), (rest, (2,)), (rest, (0, 1))))
+
+    @pl.when(me == 0)
+    def _():
+        side_k[...] = k_rows[:, half * slab : inner * slab]
+        side_v[...] = v_rows[:, half * slab : inner * slab]
 
     for other in range(outer - 1):
 
@@ -571,21 +603,86 @@
             moved = moved + jnp.dot(restore, rest, preferred_element_type=jnp.float32)
         return moved.reshape(2, tokens, slab)
 
-    def return_near(index, states):
-        for pair, state in enumerate(states):
-            moved = restored(finish(state), True)
-            for step in range(2):
-                ready[index * half + 2 * pair + step] = moved[step]
-        for step in range(1, half):
-            backbound(index * half + lax.rem(me + step, half), me).start()
-        out_ref[:, columns(me)] = ready[me]
-
-    def return_apart(index, pair, state):
+    def keep_exact(index, pair, state):
+        moved = restored(finish(state), True)
+        for step in range(2):
+            ready[index * half + 2 * pair + step] = moved[step]
+
+    def send_half(index, pair, state, arrival):
         moved = restored(finish(state), False).astype(jnp.bfloat16)
         for step in range(2):
             peer = index * half + 2 * pair + step
             ready_half[peer] = moved[step]
-            crossbound(peer, me).start()
+            crossbound(peer, me, arrival).start()
+
+    head_lane = lax.broadcasted_iota(jnp.int32, (tokens, slab), 1) // width
+
+    def local_part(place):
+        first = (half + place) * 4 // inner
+        at = slice((half + place) * slab, (half + place + 1) * slab)
+        side_at = slice(place * slab, (place + 1) * slab)
+        before = row_place(square, 1, first) <= row_place(square, 0, first)
+        own = jnp.where(
+            before, jnp.where(same, jnp.where(both, math.log2(3.0), 1.0), 0.0), FLOOR_SCORE
+        )
+        table = jnp.concatenate([jnp.where(core == 1, below, FLOOR_SCORE), own], axis=1)
+        keys = jnp.concatenate([side_k[:, side_at], k_rows[:, at]], axis=0)
+        values = jnp.concatenate([side_v[:, side_at], v_rows[:, at]], axis=0)
+        state = attend_part(by_head(q_rows[:, at]), keys, values, twice(table))
+        for which in range(3):
+            local_ref[which, place] = jnp.where(
+                head_lane == 0, state[which][0:tokens], state[which][tokens:]
+            )
+
+    tile_lane = lax.broadcasted_iota(jnp.int32, (tile, slab), 1)
+    spread_row = lax.broadcasted_iota(jnp.int32, (slab, slab), 0)
+    spread_column = lax.broadcasted_iota(jnp.int32, (slab, slab), 1)
+    spread = jnp.where(
+        (spread_row // width == spread_column // width)
+        & (spread_row % (width // 4) == 0)
+        & (spread_row % width < 3 * (width // 4)),
+        1.0,
+        0.0,
+    ).astype(jnp.bfloat16)
+
+    def far_part():
+        top, total, summed = far_block(0, 0, 1)[0]
+        lane = lax.broadcasted_iota(jnp.int32, (2, tile, slab), 2)
+        top, total, summed = (
+            jnp.where(lane < width, part[0:2], part[2:4]) for part in (top, total, summed)
+        )
+        lse = top + jnp.log2(total)
+        place = lane % width // (width // 4)
+        high = lse.astype(jnp.bfloat16).astype(jnp.float32)
+        middle = (lse - high).astype(jnp.bfloat16).astype(jnp.float32)
+        low = lse - high - middle
+        packed = jnp.where(
+            place == 0, high, jnp.where(place == 1, middle, jnp.where(place == 2, low, 0.0))
+        )
+        result = summed / total
+        for peer in range(2):
+            far_out[peer, 0] = result[peer].astype(jnp.bfloat16)
+            far_out[peer, 1] = packed[peer].astype(jnp.bfloat16)
+            partbound(peer).start()
+
+    def local_join(place):
+        at = slice(place * slab, (place + 1) * slab)
+        result = far_landed[0, :, at].astype(jnp.float32)
+        lse = jnp.dot(far_landed[1, :, at], spread, preferred_element_type=jnp.float32)
+        top, total, summed = (local_ref[which, place, 0:tile] for which in range(3))
+        top, total, summed = join((top, total, summed), (lse, jnp.ones_like(lse), result))
+        local_ref[1, place, 0:tile] = total
+        local_ref[2, place, 0:tile] = summed
+
+    def local_finish(place):
+        first = (half + place) * 4 // inner
+        order = (at_row == row_place(square, 1, first)).astype(jnp.float32).astype(jnp.bfloat16)
+        result = local_ref[2, place] / local_ref[1, place]
+        coarse = result.astype(jnp.bfloat16)
+        fine = (result - coarse.astype(jnp.float32)).astype(jnp.bfloat16)
+        moved = jnp.dot(order, coarse, preferred_element_type=jnp.float32)
+        moved = moved + jnp.dot(order, fine, preferred_element_type=jnp.float32)
+        out_ref[:, (half + place) * slab : (half + place + 1) * slab] = moved
 
     drain(in_sem.at[0], (half - 1) * 2 * tile)
 
@@ -594,6 +691,16 @@
         pass_on(1, 1, rest_count)
 
     forward(side)
+
+    @pl.when(chip == 0)
+    def _():
+        @pl.when(core == 1)
+        def _():
+            drain(in_sem.at[6], 2 * tokens * half)
+
+        for place in range(half):
+            local_part(place)
+
     drain(in_sem.at[2], half * 2 * tile)
     forward(1 - side)
     drain(in_sem.at[1], (half - 1) * (3 * tokens - 2 * tile))
@@ -617,64 +724,103 @@
         apart_far = far_block(1, 0, pairs)
         for pair in range(pairs):
             keep_state(1, pair, join_tile(load_state(1, pair), apart_far[pair]))
-        return_near(
-            0, [join_tile(load_state(0, pair), near_far[pair]) for pair in range(pairs)]
-        )
+        for pair in range(pairs):
+            keep_exact(0, pair, join_tile(load_state(0, pair), near_far[pair]))
+        for step in range(1, half):
+            backbound(lax.rem(me + step, half), me).start()
+        out_ref[:, columns(me)] = ready[me]
         for pair in range(pairs):
             drain(in_sem.at[4 + pair], 4 * (tokens - tile))
-            return_apart(1, pair, join(load_state(1, pair), edge(1, pair)))
+            send_half(1, pair, join(load_state(1, pair), edge(1, pair)), 1 + me // 2)
 
     @pl.when(side == 1)
     def _():
         for pair in range(pairs):
             keep_state(1, pair, edge(1, pair))
-        def join_below():
-            drain(in_sem.at[3], 4 * (tokens - tile))
-            for pair in range(pairs):
-                keep_state(1, pair, join(load_state(1, pair), below_block(pair)))
-
-        drain(in_sem.at[4], 4 * (tokens - tile) + 2 * tokens)
-
-        first = (mine == 0) | (chip == chips - 1)
-
-        @pl.when(jnp.logical_not(first))
-        def _():
-            join_below()
-
+
+        drain(in_sem.at[4], 4 * (tokens - tile) + 2 * tile)
+        drain(in_sem.at[3], 4 * (tokens - tile))
+        for pair in range(pairs):
+            keep_state(1, pair, join(load_state(1, pair), below_block(pair)))
         wait_far()
-        return_apart(0, 0, join_tile(edge(0, 0), far_block(0, 0, 1)[0]))
-
-        def near_block():
+
+        @pl.when(mine > 0)
+        def _():
+            far_part()
+
+        def near_block(own):
+            away = 1 - own
             near_far = far_block(1, 0, pairs)
-            return_near(
-                1, [join_tile(load_state(1, pair), near_far[pair]) for pair in range(pairs)]
-            )
-
-        @pl.when(first)
-        def _():
-            join_below()
+            send_half(1, away, join_tile(load_state(1, away), near_far[away]), 0)
+            keep_exact(1, own, join_tile(load_state(1, own), near_far[own]))
+            backbound(partner, me).start()
+            out_ref[:, columns(me)] = ready[me]
 
         @pl.when(chip < chips - 1)
         def _():
-            near_block()
+            near_block(0)
 
         drain(in_sem.at[5], 2 * tokens)
-        return_apart(0, 1, join_tile(edge(0, 1), far_block(0, 1, 2)[0]))
+        send_half(0, 1, join_tile(edge(0, 1), far_block(0, 1, 2)[0]), chip - 1)
 
         @pl.when(chip == chips - 1)
         def _():
-            near_block()
-
-    there = (1 - side) * half
-    drain(back_sem.at[0], (half - 1) * 2 * tokens)
-    for pair in range(pairs):
-        drain(back_sem.at[1 + pair], 2 * tokens)
-        for step in (2 * pair, 2 * pair + 1):
-            owner = there + step
+            near_block(1)
+
+    @pl.when(side == 0)
+    def _():
+        drain(back_sem.at[0], (half - 1) * 2 * tokens)
+
+    @pl.when(side == 1)
+    def _():
+        drain(back_sem.at[0], 4 * tokens)
+        for step in range(2):
+            owner = (chips - 1 - chip + chips // 2) * 2 + step
             out_ref[:, columns(owner)] = landed[:, columns(owner)].astype(jnp.float32)
 
-    drain(send_sem.at[0], (inner - 1) * 3 * tokens)
-    drain(send_sem.at[2], (half - 1) * 2 * tokens + half * tokens)
+    @pl.when(chip == 0)
+    def _():
+        @pl.when(mine > 0)
+        def _():
+            drain(back_sem.at[1], half * 2 * tile)
+            for place in range(half):
+                local_join(place)
+
+        for place in range(half):
+            local_finish(place)
+
+    @pl.when(chip > 0)
+    def _():
+        for pair in range(pairs):
+            drain(back_sem.at[1 + pair], 2 * tokens)
+            for step in (2 * pair, 2 * pair + 1):
+                owner = (1 - side) * half + step
+                out_ref[:, columns(owner)] = landed[:, columns(owner)].astype(jnp.float32)
+
+        drain(send_sem.at[0], (inner - 1) * 3 * tokens)
+
+    sent_near = (half - 1) * 3 * tokens + half * (2 * tokens + tile)
+
+    @pl.when((chip == 0) & (core == 0))
+    def _():
+        drain(send_sem.at[0], sent_near + 2 * tokens * half)
+
+    @pl.when((chip == 0) & (core == 1))
+    def _():
+        drain(send_sem.at[0], sent_near)
+
+    @pl.when(side == 0)
+    def _():
+        drain(send_sem.at[2], (half - 1) * 2 * tokens + half * tokens)
+
+    @pl.when((side == 1) & (mine == 0))
+    def _():
+        drain(send_sem.at[2], 6 * tokens)
+
+    @pl.when((side == 1) & (mine > 0))
+    def _():
+        drain(send_sem.at[2], 6 * tokens + 4 * tile)
+
     for count in range(1, outer):
 
         @pl.when(outer - 1 - mine == count)
@@ -704,9 +850,13 @@
             pltpu.VMEM((inner, tokens, slab), jnp.float32),
             pltpu.VMEM((inner, tokens, slab), jnp.bfloat16),
             pltpu.VMEM((tokens, features), jnp.bfloat16),
+            *[pltpu.VMEM((tokens, features // 2), jnp.bfloat16)] * 2,
+            pltpu.VMEM((3, inner // 2, tokens, slab), jnp.float32),
+            pltpu.VMEM((2, 2, tile, slab), jnp.bfloat16),
+            pltpu.VMEM((2, tile, features // 2), jnp.bfloat16),
             pltpu.VMEM((inner * 2 * tokens, slab), jnp.float32),
             pltpu.SemaphoreType.DMA((3,)),
-            pltpu.SemaphoreType.DMA((4 + pairs,)),
+            pltpu.SemaphoreType.DMA((5 + pairs,)),
             pltpu.SemaphoreType.DMA((outer - 1,)),
             pltpu.SemaphoreType.DMA((1 + pairs,)),
             pltpu.SemaphoreType.DMA((3,)),

time: 18.6 us -> 17.9 us (0.962)
  the two profiles are of different devices: /device:TPU:13 before, /device:TPU:5 now
where the time goes in v4:
time: 17.9 us; the launch traced here: 17.7 us
  Pallas kernels  17 us (95%)
  local copies, waits for them, and re-layouts  0.71 us (4%)
    pallas_call x1, Pallas kernels, fused(): pl.pallas_call(partial(fused_kernel, dims), out_shape=pltpu.VMEM((tokens,...  17 us
    unnamed x1, local copies, waits for them, and re-layouts  0.71 us

profile of v4, /device:TPU:5, one launch (start us, length us, event | category | flops | bytes accessed | tf_op | source)
XLA Modules:
  0.0 17.7 jit_solution(12717720708796674377)
XLA Ops:
  0.0 17.0 %shard_map.37 = f32[64,1024]{1,0:T(8,128)S(1)} custom-call(bf16[64,1024]{1,0:T(8,128)(2,1)} %q_ref.1, bf16[64,1024]{1,0:T(8,128)(2,1)} %k_ref.1, bf16[64,1024]{1,0:T(8,128)(2,1)} %v_ref.1), custom_call_target="tpu_custom_call" | custom-call | tf_op jit(solution)/shard_map/pallas_call | solution.py:840
  17.0 0.7 %copy.5 = f32[64,1024]{1,0:T(8,128)} copy(f32[64,1024]{1,0:T(8,128)S(1)} %shard_map.37) | data formatting | bytes 524288

commit v5 on v4

--- a/solution.py
+++ b/solution.py
@@ -333,7 +333,7 @@
         if other < chips // 2:
             counter = jnp.where(jnp.abs(chip - other) > 1, 1, 0)
         else:
-            counter = jnp.where(chip > other, 1, 0)
+            counter = jnp.where((chip > other) & (mine > 0), 1, 0)
 
         @pl.when(chip != other)
         def _():
@@ -362,8 +362,9 @@
         buffers[which][me] = placed[which][:, columns(me)]
 
     adjacent = jnp.where(chip == 0, 1, 2)
-    near_count = 1 + 2 * jnp.where(side == 0, adjacent, chip)
-    rest_count = 1 + 2 * (outer - 1) + 2 * (chips - 1 - jnp.where(side == 0, adjacent, chip))
+    near_chips = jnp.where(side == 0, adjacent, jnp.where(mine == 0, chips - 1, chip))
+    near_count = 1 + 2 * near_chips
+    rest_count = 1 + 2 * (outer - 1) + 2 * (chips - 1 - near_chips)
 
     def pass_on(first, stage, count):
         @pl.when(core == first)
@@ -397,8 +398,8 @@
     def send(source, batches):
         for group, targets in batches:
             for target in targets:
-                for which in group:
-                    for other in range(2):
+                for other in range(2):
+                    for which in group:
                         arrival = arrival_of(which, source, target)
                         inbound(which, target * 2 + other, me, arrival).start()
 
@@ -450,13 +451,31 @@
 
     @pl.when(chip == 2)
     def _():
-        send(2, ((query, (0, 1)),))
+        @pl.when(mine == 0)
+        def _():
+            send(2, ((query, (0, 1)),))
+
+        @pl.when(mine > 0)
+        def _():
+            pass_on(1, 1, rest_count)
+
+        send(2, ((picks, (3,)),))
+
+        @pl.when(mine > 0)
+        def _():
+            send(2, ((query, (0, 1)),))
+
+        send(2, ((rest, (0, 1)), (query, (3,)), (rest, (3,))))
+
+        @pl.when(mine == 0)
+        def _():
+            pass_on(1, 1, rest_count)
+
+
+    @pl.when(chip == 3)
+    def _():
+        send(3, ((query, (0, 1, 2)), (rest, (2,)), (rest, (0, 1))))
         pass_on(1, 1, rest_count)
-        send(2, ((picks, (3,)), (rest, (0, 1)), (query, (3,)), (rest, (3,))))
-
-    @pl.when(chip == 3)
-    def _():
-        send(3, ((query, (0, 1, 2)), (rest, (2,)), (rest, (0, 1))))
 
     @pl.when(me == 0)
     def _():
@@ -685,10 +704,6 @@
         out_ref[:, (half + place) * slab : (half + place + 1) * slab] = moved
 
     drain(in_sem.at[0], (half - 1) * 2 * tile)
-
-    @pl.when(chip == chips - 1)
-    def _():
-        pass_on(1, 1, rest_count)
 
     forward(side)
 

time: 17.9 us -> 17.7 us (0.989)
  the two profiles are of different devices: /device:TPU:5 before, /device:TPU:25 now
where the time goes in v5:
time: 17.7 us; the launch traced here: 17.6 us
  Pallas kernels  16.9 us (95%)
  local copies, waits for them, and re-layouts  0.71 us (4%)
    pallas_call x1, Pallas kernels, fused(): pl.pallas_call(partial(fused_kernel, dims), out_shape=pltpu.VMEM((tokens,...  16.9 us
    unnamed x1, local copies, waits for them, and re-layouts  0.71 us

profile of v5, /device:TPU:25, one launch (start us, length us, event | category | flops | bytes accessed | tf_op | source)
XLA Modules:
  0.0 17.6 jit_solution(11799183068651868389)
XLA Ops:
  0.0 16.9 %shard_map.37 = f32[64,1024]{1,0:T(8,128)S(1)} custom-call(bf16[64,1024]{1,0:T(8,128)(2,1)} %q_ref.1, bf16[64,1024]{1,0:T(8,128)(2,1)} %k_ref.1, bf16[64,1024]{1,0:T(8,128)(2,1)} %v_ref.1), custom_call_target="tpu_custom_call" | custom-call | tf_op jit(solution)/shard_map/pallas_call | solution.py:855
  16.9 0.7 %copy.5 = f32[64,1024]{1,0:T(8,128)} copy(f32[64,1024]{1,0:T(8,128)S(1)} %shard_map.37) | data formatting | bytes 524288

commit v6 on v5

--- a/solution.py
+++ b/solution.py
@@ -214,7 +214,7 @@
 
 def fused_kernel(
     dims, q_ref, k_ref, v_ref, out_ref, q_held, k_held, v_held, q_rows, k_rows, v_rows, q_buf, k_buf, v_buf, far_k, far_v,
-    state_ref, ready, ready_half, landed, side_k, side_v, local_ref, far_out, far_landed,
+    state_ref, ready, ready_half, landed, side_k, side_v, local_ref, far_out, far_landed, part_out, part_landed,
     spare, send_sem, in_sem, far_sem, back_sem, held_sem, stage_sem,
 ):
     inner, outer, tokens, slab, width = dims
@@ -284,13 +284,16 @@
             device_id_type=mesh_id,
         )
 
-    def sidebound(which):
+    def apart_columns(base):
+        return slice(base * slab, (base + half) * slab)
+
+    def sidebound(which, base, peer):
         return pltpu.make_async_remote_copy(
-            src_ref=placed[which].at[:, half * slab : inner * slab],
+            src_ref=placed[which].at[:, apart_columns(base)],
             dst_ref=(side_k, side_v)[which],
             send_sem=send_sem.at[0],
             recv_sem=in_sem.at[6],
-            device_id={"inner": 1},
+            device_id={"inner": peer},
             device_id_type=mesh_id,
         )
 
@@ -301,6 +304,16 @@
             send_sem=send_sem.at[2],
             recv_sem=back_sem.at[1],
             device_id={"inner": peer},
+            device_id_type=mesh_id,
+        )
+
+    def lastbound(step):
+        return pltpu.make_async_remote_copy(
+            src_ref=part_out.at[step],
+            dst_ref=part_landed.at[:, columns(me)],
+            send_sem=send_sem.at[2],
+            recv_sem=back_sem.at[1],
+            device_id={"inner": inner - 2 + step},
             device_id_type=mesh_id,
         )
 
@@ -419,7 +432,7 @@
         @pl.when(core == 0)
         def _():
             for which in range(2):
-                sidebound(which).start()
+                sidebound(which, half, 1).start()
 
 
     @pl.when(chip == 1)
@@ -474,13 +487,21 @@
 
     @pl.when(chip == 3)
     def _():
-        send(3, ((query, (0, 1, 2)), (rest, (2,)), (rest, (0, 1))))
+        send(3, ((query, (0, 1, 2)), (rest, (2,))))
+
+        @pl.when(core == 0)
+        def _():
+            for which in range(2):
+                sidebound(which, 0, inner - 1).start()
+
         pass_on(1, 1, rest_count)
 
-    @pl.when(me == 0)
-    def _():
-        side_k[...] = k_rows[:, half * slab : inner * slab]
-        side_v[...] = v_rows[:, half * slab : inner * slab]
+    for place, base in ((0, half), (inner - 2, 0)):
+
+        @pl.when(me == place)
+        def _():
+            side_k[...] = k_rows[:, apart_columns(base)]
+            side_v[...] = v_rows[:, apart_columns(base)]
 
     for other in range(outer - 1):
 
@@ -636,9 +657,9 @@
 
     head_lane = lax.broadcasted_iota(jnp.int32, (tokens, slab), 1) // width
 
-    def local_part(place):
-        first = (half + place) * 4 // inner
-        at = slice((half + place) * slab, (half + place + 1) * slab)
+    def local_part(base, place):
+        first = (base + place) * 4 // inner
+        at = slice((base + place) * slab, (base + place + 1) * slab)
         side_at = slice(place * slab, (place + 1) * slab)
         before = row_place(square, 1, first) <= row_place(square, 0, first)
         own = jnp.where(
@@ -693,15 +714,70 @@
         local_ref[1, place, 0:tile] = total
         local_ref[2, place, 0:tile] = summed
 
-    def local_finish(place):
-        first = (half + place) * 4 // inner
+    def thirds(value):
+        high = value.astype(jnp.bfloat16).astype(jnp.float32)
+        middle = (value - high).astype(jnp.bfloat16).astype(jnp.float32)
+        return high, middle, value - high - middle
+
+    lanes = width // 4
+
+    def send_last(state):
+        top, total, summed = (part.reshape(2, 2, tokens, slab) for part in state)
+        lse = top + jnp.log2(total)
+        lane = lax.broadcasted_iota(jnp.int32, (tokens, slab), 1)
+        term = lane % lanes // (lanes // 4)
+        for step in range(2):
+            result = jnp.where(lane < width, summed[0, step], summed[1, step]) / jnp.where(
+                lane < width, total[0, step], total[1, step]
+            )
+            kept = jnp.where(lane % (2 * lanes) < lanes, lse[0, step], lse[1, step])
+            high, middle, low = thirds(kept)
+            packed = jnp.where(
+                term == 0, high, jnp.where(term == 1, middle, jnp.where(term == 2, low, 0.0))
+            )
+            group = lax.broadcasted_iota(jnp.int32, (tile, slab), 1) // (2 * lanes)
+            folded = packed[0:tile]
+            for part in range(1, 4):
+                folded = jnp.where(group == part, packed[part * tile : (part + 1) * tile], folded)
+            part_out[step, 0:tokens] = result.astype(jnp.bfloat16)
+            part_out[step, tokens : tokens + tile] = folded.astype(jnp.bfloat16)
+            lastbound(step).start()
+
+    unfold_shape = (slab, 4 * slab)
+    unfold_row = lax.broadcasted_iota(jnp.int32, unfold_shape, 0)
+    unfold_column = lax.broadcasted_iota(jnp.int32, unfold_shape, 1)
+    unfold = jnp.where(
+        (unfold_row // (2 * lanes) == unfold_column // slab)
+        & (unfold_row % (2 * lanes) // lanes == unfold_column % slab // width)
+        & (unfold_row % (lanes // 4) == 0)
+        & (unfold_row % lanes < 3 * (lanes // 4)),
+        1.0,
+        0.0,
+    ).astype(jnp.bfloat16)
+
+    def last_join(place):
+        at = slice(place * slab, (place + 1) * slab)
+        result = part_landed[0:tokens, at].astype(jnp.float32)
+        wide_lse = jnp.dot(
+            part_landed[tokens : tokens + tile, at], unfold, preferred_element_type=jnp.float32
+        )
+        lse = jnp.concatenate(
+            [wide_lse[:, part * slab : (part + 1) * slab] for part in range(4)], axis=0
+        )
+        state = [local_ref[which, place] for which in range(3)]
+        top, total, summed = join(state, (lse, jnp.ones_like(lse), result))
+        local_ref[1, place] = total
+        local_ref[2, place] = summed
+
+    def local_finish(base, place):
+        first = (base + place) * 4 // inner
         order = (at_row == row_place(square, 1, first)).astype(jnp.float32).astype(jnp.bfloat16)
         result = local_ref[2, place] / local_ref[1, place]
         coarse = result.astype(jnp.bfloat16)
         fine = (result - coarse.astype(jnp.float32)).astype(jnp.bfloat16)
         moved = jnp.dot(order, coarse, preferred_element_type=jnp.float32)
         moved = moved + jnp.dot(order, fine, preferred_element_type=jnp.float32)
-        out_ref[:, (half + place) * slab : (half + place + 1) * slab] = moved
+        out_ref[:, (base + place) * slab : (base + place + 1) * slab] = moved
 
     drain(in_sem.at[0], (half - 1) * 2 * tile)
 
@@ -714,10 +790,20 @@
             drain(in_sem.at[6], 2 * tokens * half)
 
         for place in range(half):
-            local_part(place)
+            local_part(half, place)
 
     drain(in_sem.at[2], half * 2 * tile)
     forward(1 - side)
+
+    @pl.when(chip == chips - 1)
+    def _():
+        @pl.when(core == 1)
+        def _():
+            drain(in_sem.at[6], 2 * tokens * half)
+
+        for place in range(half):
+            local_part(0, place)
+
     drain(in_sem.at[1], (half - 1) * (3 * tokens - 2 * tile))
 
     def wait_far():
@@ -744,9 +830,19 @@
         for step in range(1, half):
             backbound(lax.rem(me + step, half), me).start()
         out_ref[:, columns(me)] = ready[me]
-        for pair in range(pairs):
-            drain(in_sem.at[4 + pair], 4 * (tokens - tile))
-            send_half(1, pair, join(load_state(1, pair), edge(1, pair)), 1 + me // 2)
+        drain(in_sem.at[4], 4 * (tokens - tile))
+        send_last(
+            join(
+                load_state(1, 1),
+                attend_part(
+                    pair_queries(1, 1),
+                    span_of(k_buf, half, half + 2),
+                    span_of(v_buf, half, half + 2),
+                    below_pair,
+                ),
+            )
+        )
+        send_half(1, 0, join(load_state(1, 0), edge(1, 0)), 1 + me // 2)
 
     @pl.when(side == 1)
     def _():
@@ -802,9 +898,17 @@
                 local_join(place)
 
         for place in range(half):
-            local_finish(place)
-
-    @pl.when(chip > 0)
+            local_finish(half, place)
+
+    @pl.when(chip == chips - 1)
+    def _():
+        drain(back_sem.at[1], half * (tokens + tile))
+        for place in range(half):
+            last_join(place)
+        for place in range(half):
+            local_finish(0, place)
+
+    @pl.when((chip > 0) & (chip < chips - 1))
     def _():
         for pair in range(pairs):
             drain(back_sem.at[1 + pair], 2 * tokens)
@@ -824,9 +928,19 @@
     def _():
         drain(send_sem.at[0], sent_near)
 
+    sent_last = (half - 1) * 3 * tokens + half * (tokens + 2 * tile)
+
+    @pl.when((chip == chips - 1) & (core == 0))
+    def _():
+        drain(send_sem.at[0], sent_last + 2 * tokens * half)
+
+    @pl.when((chip == chips - 1) & (core == 1))
+    def _():
+        drain(send_sem.at[0], sent_last)
+
     @pl.when(side == 0)
     def _():
-        drain(send_sem.at[2], (half - 1) * 2 * tokens + half * tokens)
+        drain(send_sem.at[2], (half - 1) * 2 * tokens + half * tokens + 2 * tile)
 
     @pl.when((side == 1) & (mine == 0))
     def _():
@@ -869,6 +983,8 @@
             pltpu.VMEM((3, inner // 2, tokens, slab), jnp.float32),
             pltpu.VMEM((2, 2, tile, slab), jnp.bfloat16),
             pltpu.VMEM((2, tile, features // 2), jnp.bfloat16),
+            pltpu.VMEM((2, tokens + tile, slab), jnp.bfloat16),
+            pltpu.VMEM((tokens + tile, features // 2), jnp.bfloat16),
             pltpu.VMEM((inner * 2 * tokens, slab), jnp.float32),
             pltpu.SemaphoreType.DMA((3,)),
             pltpu.SemaphoreType.DMA((5 + pairs,)),

time: 17.7 us -> 17 us (0.960)
  the two profiles are of different devices: /device:TPU:25 before, /device:TPU:13 now
where the time goes in v6:
time: 17 us; the launch traced here: 16.9 us
  Pallas kernels  16.1 us (95%)
  local copies, waits for them, and re-layouts  0.71 us (4%)
    pallas_call x1, Pallas kernels, fused(): pl.pallas_call(partial(fused_kernel, dims), out_shape=pltpu.VMEM((tokens,...  16.1 us
    unnamed x1, local copies, waits for them, and re-layouts  0.71 us

profile of v6, /device:TPU:13, one launch (start us, length us, event | category | flops | bytes accessed | tf_op | source)
XLA Modules:
  0.0 16.9 jit_solution(8370141259234923911)
XLA Ops:
  0.0 16.1 %shard_map.37 = f32[64,1024]{1,0:T(8,128)S(1)} custom-call(bf16[64,1024]{1,0:T(8,128)(2,1)} %q_ref.1, bf16[64,1024]{1,0:T(8,128)(2,1)} %k_ref.1, bf16[64,1024]{1,0:T(8,128)(2,1)} %v_ref.1), custom_call_target="tpu_custom_call" | custom-call | tf_op jit(solution)/shard_map/pallas_call | solution.py:969
  16.1 0.7 %copy.5 = f32[64,1024]{1,0:T(8,128)} copy(f32[64,1024]{1,0:T(8,128)S(1)} %shard_map.37) | data formatting | bytes 524288

commit v7 on v6

--- a/solution.py
+++ b/solution.py
@@ -454,7 +454,7 @@
     def _():
         send(0, ((query, (1,)),))
         pass_on(1, 1, rest_count)
-        send(0, ((picks, (3, 2)), ((pick_q,) + rest, (3, 2))))
+        send(0, ((picks, (3, 2)), ((pick_q,) + rest, (2, 3))))
 
     @pl.when(chip == 1)
     def _():
@@ -867,12 +867,12 @@
             backbound(partner, me).start()
             out_ref[:, columns(me)] = ready[me]
 
-        @pl.when(chip < chips - 1)
-        def _():
-            near_block(0)
-
         drain(in_sem.at[5], 2 * tokens)
         send_half(0, 1, join_tile(edge(0, 1), far_block(0, 1, 2)[0]), chip - 1)
+
+        @pl.when(chip < chips - 1)
+        def _():
+            near_block(0)
 
         @pl.when(chip == chips - 1)
         def _():

time: 17 us -> 16.7 us (0.982)
  the two profiles are of different devices: /device:TPU:13 before, /device:TPU:5 now
where the time goes in v7:
time: 16.7 us; the launch traced here: 16.4 us
  Pallas kernels  15.7 us (94%)
  local copies, waits for them, and re-layouts  0.71 us (4%)
    pallas_call x1, Pallas kernels, fused(): pl.pallas_call(partial(fused_kernel, dims), out_shape=pltpu.VMEM((tokens,...  15.7 us
    unnamed x1, local copies, waits for them, and re-layouts  0.71 us

profile of v7, /device:TPU:5, one launch (start us, length us, event | category | flops | bytes accessed | tf_op | source)
XLA Modules:
  0.0 16.4 jit_solution(16966646580597819229)
XLA Ops:
  0.0 15.7 %shard_map.37 = f32[64,1024]{1,0:T(8,128)S(1)} custom-call(bf16[64,1024]{1,0:T(8,128)(2,1)} %q_ref.1, bf16[64,1024]{1,0:T(8,128)(2,1)} %k_ref.1, bf16[64,1024]{1,0:T(8,128)(2,1)} %v_ref.1), custom_call_target="tpu_custom_call" | custom-call | tf_op jit(solution)/shard_map/pallas_call | solution.py:969
  15.7 0.7 %copy.5 = f32[64,1024]{1,0:T(8,128)} copy(f32[64,1024]{1,0:T(8,128)S(1)} %shard_map.37) | data formatting | bytes 524288

commit v8 on v7

--- a/solution.py
+++ b/solution.py
@@ -341,7 +341,7 @@
 
     greet({"inner": partner})
     for step in range(1, outer):
-        greet({"inner": chip * 2 + 1, "outer": lax.rem(mine + step, outer)})
+        greet({"inner": chip * 2, "outer": lax.rem(mine + step, outer)})
     for other in range(chips):
         if other < chips // 2:
             counter = jnp.where(jnp.abs(chip - other) > 1, 1, 0)
@@ -350,7 +350,7 @@
 
         @pl.when(chip != other)
         def _():
-            greet({"inner": other * 2 + counter})
+            greet({"inner": other * 2 + 1 - counter})
 
     def row_place(shape, axis, first):
         row = lax.broadcasted_iota(jnp.int32, shape, axis)
@@ -422,7 +422,7 @@
 
     place_rows(0)
     place_rows(1)
-    pass_on(0, 0, near_count)
+    pass_on(1, 0, near_count)
     send_partner(picks + rest)
 
     @pl.when(chip == 0)
@@ -453,13 +453,13 @@
     @pl.when(chip == 0)
     def _():
         send(0, ((query, (1,)),))
-        pass_on(1, 1, rest_count)
+        pass_on(0, 1, rest_count)
         send(0, ((picks, (3, 2)), ((pick_q,) + rest, (2, 3))))
 
     @pl.when(chip == 1)
     def _():
         send(1, ((query, (0,)),))
-        pass_on(1, 1, rest_count)
+        pass_on(0, 1, rest_count)
         send(1, ((picks, (3,)), (rest, (3,)), ((rest_v,), (2,)), (query, (3, 2))))
 
     @pl.when(chip == 2)
@@ -470,7 +470,7 @@
 
         @pl.when(mine > 0)
         def _():
-            pass_on(1, 1, rest_count)
+            pass_on(0, 1, rest_count)
 
         send(2, ((picks, (3,)),))
 
@@ -482,7 +482,7 @@
 
         @pl.when(mine == 0)
         def _():
-            pass_on(1, 1, rest_count)
+            pass_on(0, 1, rest_count)
 
 
     @pl.when(chip == 3)
@@ -494,7 +494,7 @@
             for which in range(2):
                 sidebound(which, 0, inner - 1).start()
 
-        pass_on(1, 1, rest_count)
+        pass_on(0, 1, rest_count)
 
     for place, base in ((0, half), (inner - 2, 0)):
 

time: 16.7 us -> 16.6 us (level)
  no operation moved by 1% of the time
where the time goes in v8:
time: 16.6 us; the launch traced here: 16.4 us
  Pallas kernels  15.7 us (95%)
  local copies, waits for them, and re-layouts  0.71 us (4%)
    pallas_call x1, Pallas kernels, fused(): pl.pallas_call(partial(fused_kernel, dims), out_shape=pltpu.VMEM((tokens,...  15.7 us
    unnamed x1, local copies, waits for them, and re-layouts  0.71 us

profile of v8, /device:TPU:5, one launch (start us, length us, event | category | flops | bytes accessed | tf_op | source)
XLA Modules:
  0.0 16.4 jit_solution(16949083714831316886)
XLA Ops:
  0.0 15.7 %shard_map.37 = f32[64,1024]{1,0:T(8,128)S(1)} custom-call(bf16[64,1024]{1,0:T(8,128)(2,1)} %q_ref.1, bf16[64,1024]{1,0:T(8,128)(2,1)} %k_ref.1, bf16[64,1024]{1,0:T(8,128)(2,1)} %v_ref.1), custom_call_target="tpu_custom_call" | custom-call | tf_op jit(solution)/shard_map/pallas_call | solution.py:969
  15.7 0.7 %copy.5 = f32[64,1024]{1,0:T(8,128)} copy(f32[64,1024]{1,0:T(8,128)S(1)} %shard_map.37) | data formatting | bytes 524288

commit v9 on v8

--- a/solution.py
+++ b/solution.py
@@ -421,8 +421,25 @@
             inbound(which, partner, me, 0 if which in picks else 1).start()
 
     place_rows(0)
-    place_rows(1)
+
+    @pl.when(side == 0)
+    def _():
+        place_rows(1)
+
     pass_on(1, 0, near_count)
+
+    @pl.when(chip == 2)
+    def _():
+        send(2, (((pick_k,), (0, 1)),))
+
+    @pl.when(chip == 3)
+    def _():
+        send(3, (((pick_k,), (0, 1, 2)),))
+
+    @pl.when(side == 1)
+    def _():
+        place_rows(1)
+
     send_partner(picks + rest)
 
     @pl.when(chip == 0)
@@ -441,11 +458,11 @@
 
     @pl.when(chip == 2)
     def _():
-        send(2, ((picks, (0, 1)),))
+        send(2, (((pick_v,), (0, 1)),))
 
     @pl.when(chip == 3)
     def _():
-        send(3, ((picks, (0, 1, 2)),))
+        send(3, (((pick_v,), (0, 1, 2)),))
 
     place_rows(2)
     send_partner(query)

time: 16.6 us -> 16.6 us (level)
  no operation moved by 1% of the time
where the time goes in v9:
time: 16.6 us; the launch traced here: 16.4 us
  Pallas kernels  15.7 us (95%)
  local copies, waits for them, and re-layouts  0.71 us (4%)
    pallas_call x1, Pallas kernels, fused(): pl.pallas_call(partial(fused_kernel, dims), out_shape=pltpu.VMEM((tokens,...  15.7 us
    unnamed x1, local copies, waits for them, and re-layouts  0.71 us

profile of v9, /device:TPU:5, one launch (start us, length us, event | category | flops | bytes accessed | tf_op | source)
XLA Modules:
  0.0 16.4 jit_solution(16604598962822659120)
XLA Ops:
  0.0 15.7 %shard_map.37 = f32[64,1024]{1,0:T(8,128)S(1)} custom-call(bf16[64,1024]{1,0:T(8,128)(2,1)} %q_ref.1, bf16[64,1024]{1,0:T(8,128)(2,1)} %k_ref.1, bf16[64,1024]{1,0:T(8,128)(2,1)} %v_ref.1), custom_call_target="tpu_custom_call" | custom-call | tf_op jit(solution)/shard_map/pallas_call | solution.py:986
  15.7 0.7 %copy.5 = f32[64,1024]{1,0:T(8,128)} copy(f32[64,1024]{1,0:T(8,128)S(1)} %shard_map.37) | data formatting | bytes 524288

commit v10 on v8

--- a/solution.py
+++ b/solution.py
@@ -235,7 +235,7 @@
     held = (k_held, v_held, q_held)
     placed = (k_rows, v_rows, q_rows)
     buffers = (k_buf, v_buf, q_buf)
-    pick_k, pick_v, rest_k, rest_v, whole_q, pick_q = range(6)
+    pick_k, pick_v, rest_k, rest_v, whole_q, pick_q, rest_q = range(7)
     pieces = (
         (0, 0, tile),
         (1, 0, tile),
@@ -243,6 +243,7 @@
         (1, tile, tokens),
         (2, 0, tokens),
         (2, 0, tile),
+        (2, tile, tokens),
     )
 
     def columns(index):
@@ -404,9 +405,9 @@
             return 1
         if target < low:
             return 3 if which == whole_q else 4 + source % low
-        if source == 0:
+        if source == 0 or which == pick_q:
             return 4
-        return 5 if which == whole_q else 3
+        return 5 if which == rest_q else 3
 
     def send(source, batches):
         for group, targets in batches:
@@ -458,9 +459,9 @@
 
     @pl.when(chip == 1)
     def _():
-        send(1, ((query, (0,)),))
+        send(1, (((pick_q,), (2,)), (query, (0,))))
         pass_on(0, 1, rest_count)
-        send(1, ((picks, (3,)), (rest, (3,)), ((rest_v,), (2,)), (query, (3, 2))))
+        send(1, ((picks + (pick_q,), (3,)), (rest, (3,)), ((rest_v,), (2,)), ((rest_q,), (3, 2))))
 
     @pl.when(chip == 2)
     def _():
@@ -685,8 +686,19 @@
         0.0,
     ).astype(jnp.bfloat16)
 
+    def keep_far(state):
+        for which in range(3):
+            state_ref[which, 0, 1, 0 : 4 * tile] = state[which].reshape(4 * tile, slab)
+
+    def kept_far():
+        return [
+            state_ref[which, 0, 1, 0 : 4 * tile].reshape(4, tile, slab) for which in range(3)
+        ]
+
     def far_part():
-        top, total, summed = far_block(0, 0, 1)[0]
+        first_far, second_far = far_block(0, 0, pairs)
+        keep_far(second_far)
+        top, total, summed = first_far
         lane = lax.broadcasted_iota(jnp.int32, (2, tile, slab), 2)
         top, total, summed = (
             jnp.where(lane < width, part[0:2], part[2:4]) for part in (top, total, summed)
@@ -849,7 +861,7 @@
         for pair in range(pairs):
             keep_state(1, pair, edge(1, pair))
 
-        drain(in_sem.at[4], 4 * (tokens - tile) + 2 * tile)
+        drain(in_sem.at[4], 4 * tokens)
         drain(in_sem.at[3], 4 * (tokens - tile))
         for pair in range(pairs):
             keep_state(1, pair, join(load_state(1, pair), below_block(pair)))
@@ -858,6 +870,11 @@
         @pl.when(mine > 0)
         def _():
             far_part()
+
+        @pl.when(mine == 0)
+        def _():
+            nothing = jnp.zeros((4, tile, slab), jnp.float32)
+            keep_far([nothing + FLOOR_SCORE, nothing, nothing])
 
         def near_block(own):
             away = 1 - own
@@ -867,8 +884,8 @@
             backbound(partner, me).start()
             out_ref[:, columns(me)] = ready[me]
 
-        drain(in_sem.at[5], 2 * tokens)
-        send_half(0, 1, join_tile(edge(0, 1), far_block(0, 1, 2)[0]), chip - 1)
+        drain(in_sem.at[5], 2 * (tokens - tile))
+        send_half(0, 1, join_tile(edge(0, 1), kept_far()), chip - 1)
 
         @pl.when(chip < chips - 1)
         def _():

time: 16.6 us -> 16.5 us (level)
  no operation moved by 1% of the time
where the time goes in v10:
time: 16.5 us; the launch traced here: 16.4 us
  Pallas kernels  15.7 us (95%)
  local copies, waits for them, and re-layouts  0.71 us (4%)
    pallas_call x1, Pallas kernels, fused(): pl.pallas_call(partial(fused_kernel, dims), out_shape=pltpu.VMEM((tokens,...  15.7 us
    unnamed x1, local copies, waits for them, and re-layouts  0.71 us

profile of v10, /device:TPU:5, one launch (start us, length us, event | category | flops | bytes accessed | tf_op | source)
XLA Modules:
  0.0 16.4 jit_solution(8670347932880429681)
XLA Ops:
  0.0 15.7 %shard_map.37 = f32[64,1024]{1,0:T(8,128)S(1)} custom-call(bf16[64,1024]{1,0:T(8,128)(2,1)} %q_ref.1, bf16[64,1024]{1,0:T(8,128)(2,1)} %k_ref.1, bf16[64,1024]{1,0:T(8,128)(2,1)} %v_ref.1), custom_call_target="tpu_custom_call" | custom-call | tf_op jit(solution)/shard_map/pallas_call | solution.py:986
  15.7 0.7 %copy.5 = f32[64,1024]{1,0:T(8,128)} copy(f32[64,1024]{1,0:T(8,128)S(1)} %shard_map.37) | data formatting | bytes 524288
